TPU v7x, 32 devices: a whole 2x2x4 slice. The times are simulated.
32 devices in a mesh: dp: 2 (over y), row: 4 (over x, core), col: 4 (over z).
Axes of the slice: x: 2, y: 2, z: 4, core: 2. Of those that a mesh axis runs over, the one named last changes fastest.
Arguments:
- tokens: bfloat16 [2048, 8192], P(('dp', 'col'), 'row'), may hold values from -6 to 6
- frozen_weight: bfloat16 [8192, 8192], P('row', 'col'), may hold values from -0.0625 to 0.0625
- input_adapter_factor: bfloat16 [16, 8192], P(None, 'row'), may hold values from -0.0625 to 0.0625
- output_adapter_factor: bfloat16 [16, 8192], P(None, 'col'), may hold values from -1.5 to 1.5
- magnitude: float32 [8192], P('col'), may hold values from 0.5 to 2
- cotangent: bfloat16 [2048, 8192], P(('dp', 'row'), 'col'), may hold values from -6 to 6
- sequence_lengths: int32 [2, 8], P('dp'), may hold values from 1 to 512, 1024 in all within a row
Outputs:
- projected: bfloat16 [2048, 8192], P(('dp', 'row'), 'col')
- grad_mag: float32 [8192], P('col')
- input_factor_gradient: float32 [16, 8192], P(None, 'row')
- grad_b: float32 [16, 8192], P(None, 'col')
Inputs may be any that keep to these rules, and one draw needn't show every extreme that they name: `sequence_lengths`: each group's 8 lengths sum to 1024, and one of them is exactly 512.
All inputs are finite; a program needn't handle non-finite values.
Results may differ from a plain program's by a relative error of at most 0.0052.
Values may be sent and summed in bfloat16 or wider, within the bound.
A program may use at most 64 MiB of HBM per device.

v0:
```python
import functools

import jax
import jax.numpy as jnp
from jax import lax
from jax.experimental import pallas as pl
from jax.experimental.pallas import tpu as pltpu
from jax.sharding import PartitionSpec as P

norm_eps = 1e-06
highest_precision = lax.Precision.HIGHEST
MESH = pl.DeviceIdType.MESH
LANES = 128
VMEM_LIMIT = 60 * 1024 * 1024


def contract_product(left, right, left_dim, right_dim):
    return lax.dot_general(
        left, right, (((left_dim,), (right_dim,)), ((), ())), preferred_element_type=jnp.float32
    )


def column_tiles(width, tile):
    return [(start, min(tile, width - start)) for start in range(0, width, tile)]


def adapter_kernel(
    D, C, R, S,
    tok, w_hbm, a_ref, b_ref, magnitude, cot_hbm, lengths,
    projected, grad_mag, factor_grad, grad_b,
    wx, gath, sb, pin, xin, pb, st_in, apad, bpad, acc, pg, cot, row_weight, down_all,
    scale_in, back_in, bsum, bsum_all, box1, fsum, box2,
    load_sem, gsend, grecv, ssend, precv, xrecv, stsend, strecv,
    sc_send, sc_recv, bk_send, bk_recv, r1a, r1b, r1c, r1d, r2a, r2b, r2c, r2d,
):
    z = lax.axis_index("col")
    r = lax.axis_index("row")
    d = lax.axis_index("dp")
    p, q = r // 2, r % 2
    pairs = R // 2
    sub, features = tok.shape[1], tok.shape[2]
    cols = w_hbm.shape[1]
    rank_rows = a_ref.shape[0]
    units = C * S
    block_units = units // R
    block_rows = block_units * sub
    tiles = column_tiles(cols, 512)
    feature_tiles = column_tiles(features, 512)
    f32, bf16 = jnp.float32, jnp.bfloat16

    load_w = pltpu.make_async_copy(w_hbm, wx, load_sem.at[0])
    load_c = pltpu.make_async_copy(cot_hbm, cot, load_sem.at[1])
    load_w.start()
    load_c.start()

    g1, g2 = D * R, D * C
    me1, me2 = d * R + r, d * C + z

    def device1(i):
        peer = (me1 + i) % g1
        return {"dp": peer // R, "row": peer % R}

    def device2(i):
        peer = (me2 + i) % g2
        return {"dp": peer // C, "col": peer % C}

    def loop(n, body):
        def turn(i, carry):
            body(i)
            return carry

        lax.fori_loop(1, n, turn, 0)

    barrier = pltpu.get_barrier_semaphore()
    loop(g1, lambda i: pl.semaphore_signal(barrier, inc=1, device_id=device1(i), device_id_type=MESH))
    loop(g2, lambda i: pl.semaphore_signal(barrier, inc=1, device_id=device2(i), device_id_type=MESH))
    pl.semaphore_wait(barrier, g1 + g2 - 2)

    def hop(src, u, direction):
        target = z - 1 if direction == 0 else z + 1
        return pltpu.make_async_remote_copy(
            src_ref=src, dst_ref=gath.at[u], send_sem=gsend.at[direction, u],
            recv_sem=grecv.at[u], device_id={"col": target}, device_id_type=MESH,
        )

    for s in range(S):
        @pl.when(z > 0)
        def _():
            hop(tok.at[s], z * S + s, 0).start()

        @pl.when(z < C - 1)
        def _():
            hop(tok.at[s], z * S + s, 1).start()

    a = a_ref[...]
    apad[...] = jnp.zeros_like(apad)
    bpad[...] = jnp.zeros_like(bpad)
    apad[0:rank_rows, :] = a
    bpad[0:rank_rows, :] = b_ref[...]
    position = r * block_rows + lax.broadcasted_iota(jnp.int32, (block_rows, LANES), 0)
    weights = jnp.zeros((block_rows, LANES), f32)
    start_row = 0
    for i in range(lengths.shape[1]):
        length = lengths[0, i]
        end_row = start_row + length
        inverse = 1.0 / jnp.full((1, LANES), length, jnp.int32).astype(f32)
        weights = jnp.where((position >= start_row) & (position < end_row), inverse, weights)
        start_row = end_row
    row_weight[...] = weights

    load_w.wait()
    load_c.wait()

    gram = contract_product(a, a, 1, 1)
    for start, width in tiles:
        span = pl.ds(start, width)
        st_in[r, 0:rank_rows, span] = jnp.dot(
            a, wx[:, span], preferred_element_type=f32
        ) + jnp.dot(
            gram, b_ref[:, span].astype(f32),
            precision=highest_precision, preferred_element_type=f32,
        )
        st_in[r, rank_rows:rank_rows + 8, span] = jnp.zeros((8, width), f32)
    depth = 256

    def norm_step(i, carry):
        rows = pl.ds(pl.multiple_of(i * depth, depth), depth)
        for start, width in tiles:
            span = pl.ds(start, width)
            merged = wx[rows, span].astype(f32) + contract_product(apad[:, rows], bpad[:, span], 0, 0)
            st_in[r, rank_rows:rank_rows + 1, span] += jnp.sum(merged * merged, axis=0, keepdims=True)
        return carry

    lax.fori_loop(0, features // depth, norm_step, 0)

    def stat_copy(i, piece):
        return pltpu.make_async_remote_copy(
            src_ref=st_in.at[piece], dst_ref=st_in.at[piece], send_sem=stsend.at[i],
            recv_sem=strecv.at[i], device_id={"row": (r + i) % R}, device_id_type=MESH,
        )

    near = jnp.minimum(z, C - 1 - z)

    def place(k):
        j = k - S
        both = j < 2 * near * S
        rest = j - 2 * near * S
        distance = jnp.where(both, j // (2 * S) + 1, near + 1 + rest // S)
        s = jnp.where(both, (j % (2 * S)) // 2, rest % S)
        leftward = jnp.where(both, j % 2 == 0, z > C - 1 - z)
        chunk = jnp.where(leftward, z - distance, z + distance)
        own = k < S
        return jnp.where(own, z, chunk), jnp.where(own, k, s)

    def pair_copy(u):
        return pltpu.make_async_remote_copy(
            src_ref=sb.at[u], dst_ref=pin.at[u], send_sem=ssend.at[u], recv_sem=precv.at[u],
            device_id={"row": p * 2 + (1 - q)}, device_id_type=MESH,
        )

    def far_copy(u, owner_pair):
        return pltpu.make_async_remote_copy(
            src_ref=sb.at[u], dst_ref=xin.at[p, u % block_units], send_sem=ssend.at[u],
            recv_sem=xrecv.at[p, u % block_units],
            device_id={"row": owner_pair * 2 + q}, device_id_type=MESH,
        )

    def multiply(k):
        c, s = place(k)
        u = c * S + s
        owner = u // block_units

        @pl.when(k < S)
        def _():
            gath[u] = tok[s]

        @pl.when(k >= S)
        def _():
            hop(gath.at[u], u, 0).wait_recv()

            @pl.when((c < z) & (z < C - 1))
            def _():
                hop(gath.at[u], u, 1).start()

            @pl.when((c > z) & (z > 0))
            def _():
                hop(gath.at[u], u, 0).start()

        slot = k % 2
        for start, width in tiles:
            span = pl.ds(start, width)
            pb[slot, :, span] = jnp.dot(gath[u], wx[:, span], preferred_element_type=f32)
        pb[slot, :, pl.ds(cols, LANES)] = contract_product(gath[u], apad[...], 1, 1)

        @pl.when(owner % 2 != q)
        def _():
            sb[u] = pb[slot].astype(bf16)
            pair_copy(u).start()

    def combine(k):
        c, s = place(k)
        u = c * S + s
        owner = u // block_units
        slot = k % 2

        @pl.when(owner % 2 == q)
        def _():
            pair_copy(u).wait_recv()
            total = pb[slot] + pin[u].astype(f32)

            @pl.when(owner // 2 == p)
            def _():
                acc[u % block_units] = total

            @pl.when(owner // 2 != p)
            def _():
                sb[u] = total.astype(bf16)
                far_copy(u, owner // 2).start()

    def step(k, carry):
        @pl.when(k < units)
        def _():
            multiply(k)

        @pl.when(k == 0)
        def _():
            for i in range(1, R):
                stat_copy(i, r).start()

        @pl.when(k > 0)
        def _():
            combine(k - 1)

        return carry

    lax.fori_loop(0, units + 1, step, 0)

    for i in range(1, R):
        stat_copy(i, (r - i + R) % R).wait_recv()
    stats = st_in[0]
    for i in range(1, R):
        stats = stats + st_in[i]
    merged_factor = stats[0:rank_rows]
    col_norm = jnp.sqrt(stats[rank_rows:rank_rows + 1] + norm_eps)
    col_scale = magnitude[...] / col_norm
    scale_in[me1] = jnp.zeros((1, cols), f32)

    def finish(v, carry):
        for i in range(1, pairs):
            other = (p + i) % pairs
            pltpu.make_async_remote_copy(
                src_ref=sb.at[v], dst_ref=xin.at[other, v], send_sem=ssend.at[v],
                recv_sem=xrecv.at[other, v], device_id={"row": other * 2 + q}, device_id_type=MESH,
            ).wait_recv()
            acc[v] += xin[other, v].astype(f32)
        rows = pl.ds(pl.multiple_of(v * sub, sub), sub)
        down = acc[v, :, pl.ds(cols, LANES)].astype(bf16)
        down_all[rows, :] = down
        weight = row_weight[rows, 0:1]
        for start, width in tiles:
            span = pl.ds(start, width)
            scale = col_scale[:, start:start + width]
            query = acc[v, :, span] + jnp.dot(down, bpad[:, span], preferred_element_type=f32)
            projected[rows, span] = (query * scale).astype(bf16)
            grad_out = cot[rows, span].astype(f32) * weight
            scale_in[me1, :, span] += jnp.sum(grad_out * query, axis=0, keepdims=True)
            pg[rows, span] = (grad_out * scale).astype(bf16)
        return carry

    lax.fori_loop(0, block_units, finish, 0)

    def scale_copy(i, piece):
        return pltpu.make_async_remote_copy(
            src_ref=scale_in.at[piece], dst_ref=scale_in.at[piece], send_sem=sc_send.at[i],
            recv_sem=sc_recv.at[i], device_id=device1(i), device_id_type=MESH,
        )

    def back_copy(i, piece):
        return pltpu.make_async_remote_copy(
            src_ref=back_in.at[piece], dst_ref=back_in.at[piece], send_sem=bk_send.at[i],
            recv_sem=bk_recv.at[i], device_id={"row": (r + i) % R}, device_id_type=MESH,
        )

    back_in[r] = contract_product(b_ref[...], pg[...], 1, 1).astype(bf16)
    loop(g1, lambda i: scale_copy(i, me1).start())
    for i in range(1, R):
        back_copy(i, r).start()

    def group_sum(g, me, device, src, box, out, s1, r1, s2, r2):
        width = max(LANES, src.shape[1] // g)
        pieces = src.shape[1] // width

        def part(j):
            return pl.ds(pl.multiple_of(j * width, width), width)

        def scatter(i):
            return pltpu.make_async_remote_copy(
                src_ref=src.at[:, part((me + i) % g % pieces)], dst_ref=box.at[i],
                send_sem=s1.at[i], recv_sem=r1.at[i], device_id=device(i), device_id_type=MESH,
            )

        def spread(i, j):
            return pltpu.make_async_remote_copy(
                src_ref=out.at[:, part(j % pieces)], dst_ref=out.at[:, part(j % pieces)],
                send_sem=s2.at[i], recv_sem=r2.at[i], device_id=device(i), device_id_type=MESH,
            )

        def to_owner(i, action):
            @pl.when((me + i) % g < pieces)
            def _():
                action(scatter(i))

        def from_owner(i, action):
            @pl.when((me - i + g) % g < pieces)
            def _():
                action(spread(i, (me - i + g) % g))

        def begin():
            loop(g, lambda i: to_owner(i, lambda copy: copy.start()))

        def middle():
            @pl.when(me < pieces)
            def _():
                def add(i, total):
                    scatter(i).wait_recv()
                    return total + box[i]

                out[:, part(me % pieces)] = lax.fori_loop(1, g, add, src[:, part(me % pieces)])
                loop(g, lambda i: spread(i, me).start())

        def end():
            loop(g, lambda i: from_owner(i, lambda copy: copy.wait_recv()))

        def drain():
            loop(g, lambda i: to_owner(i, lambda copy: copy.wait_send()))

            @pl.when(me < pieces)
            def _():
                loop(g, lambda i: spread(i, me).wait_send())

        return begin, middle, end, drain

    begin1, middle1, end1, drain1 = group_sum(
        g1, me1, device1, bsum, box1, bsum_all, r1a, r1b, r1c, r1d
    )
    begin2, middle2, end2, drain2 = group_sum(
        g2, me2, device2, fsum, box2, factor_grad, r2a, r2b, r2c, r2d
    )
    for start, width in tiles:
        span = pl.ds(start, width)
        bsum[:, span] = contract_product(down_all[...], pg[:, span], 0, 0)[0:rank_rows]
    begin1()

    for i in range(1, R):
        back_copy(i, (r - i + R) % R).wait_recv()
    for start, width in feature_tiles:
        span = pl.ds(start, width)
        term = jnp.zeros((rank_rows, width), f32)
        for j in range(R):
            block = gath[j * block_units:(j + 1) * block_units, :, span].reshape(block_rows, width)
            term = term + jnp.dot(back_in[j], block, preferred_element_type=f32)
        fsum[:, span] = term

    loop(g1, lambda i: scale_copy(i, (me1 - i + g1) % g1).wait_recv())
    scale_grad = scale_in[0]
    for j in range(1, g1):
        scale_grad = scale_grad + scale_in[j]
    grad_mag[...] = scale_grad / col_norm
    coefficient = -scale_grad * magnitude[...] / (col_norm * col_norm * col_norm)
    scaled = (b_ref[...].astype(f32) * coefficient).astype(bf16)
    cross = contract_product(scaled, b_ref[...], 1, 1)
    for index, (start, width) in enumerate(feature_tiles):
        @pl.when(d == index % D)
        def _():
            span = pl.ds(start, width)
            fsum[:, span] += contract_product(scaled, wx[span, :], 1, 1) + jnp.dot(
                cross, a_ref[:, span].astype(f32),
                precision=highest_precision, preferred_element_type=f32,
            )
    begin2()
    middle1()
    middle2()
    end1()
    grad_b[...] = bsum_all[...] + merged_factor * coefficient
    end2()

    drain1()
    drain2()
    loop(g1, lambda i: scale_copy(i, me1).wait_send())
    for i in range(1, R):
        stat_copy(i, r).wait_send()
        back_copy(i, r).wait_send()

    def drain(u, carry):
        c = u // S
        owner = u // block_units

        @pl.when((owner % 2 != q) | (owner // 2 != p))
        def _():
            pair_copy(u).wait_send()

        @pl.when((c <= z) & (z < C - 1))
        def _():
            hop(gath.at[u], u, 1).wait_send()

        @pl.when((c >= z) & (z > 0))
        def _():
            hop(gath.at[u], u, 0).wait_send()

        return carry

    lax.fori_loop(0, units, drain, 0)


def per_device(
    tokens,
    frozen_weight,
    input_adapter_factor,
    output_adapter_factor,
    magnitude,
    cotangent,
    sequence_lengths,
):
    D, C, R = lax.axis_size("dp"), lax.axis_size("col"), lax.axis_size("row")
    local_rows, features = tokens.shape
    block_rows, cols = cotangent.shape
    rank_rows = input_adapter_factor.shape[0]
    S = 4
    sub = local_rows // S
    units = C * S
    block_units = units // R
    wide = cols + LANES
    g1, g2 = D * R, D * C
    vmem = pl.BlockSpec(memory_space=pltpu.VMEM)
    smem = pl.BlockSpec(memory_space=pltpu.SMEM)
    hbm = pl.BlockSpec(memory_space=pl.ANY)
    dma = pltpu.SemaphoreType.DMA
    f32, bf16 = jnp.float32, jnp.bfloat16
    projected, grad_mag, factor_grad, grad_b = pl.pallas_call(
        functools.partial(adapter_kernel, D, C, R, S),
        out_shape=(
            jax.ShapeDtypeStruct((block_rows, cols), bf16),
            jax.ShapeDtypeStruct((1, cols), f32),
            jax.ShapeDtypeStruct((rank_rows, features), f32),
            jax.ShapeDtypeStruct((rank_rows, cols), f32),
        ),
        in_specs=[vmem, hbm, vmem, vmem, vmem, hbm, smem],
        out_specs=(vmem, vmem, vmem, vmem),
        scratch_shapes=[
            pltpu.VMEM((features, cols), bf16),
            pltpu.VMEM((units, sub, features), bf16),
            pltpu.VMEM((units, sub, wide), bf16),
            pltpu.VMEM((units, sub, wide), bf16),
            pltpu.VMEM((R // 2, block_units, sub, wide), bf16),
            pltpu.VMEM((2, sub, wide), f32),
            pltpu.VMEM((R, rank_rows + 8, cols), f32),
            pltpu.VMEM((LANES, features), bf16),
            pltpu.VMEM((LANES, cols), bf16),
            pltpu.VMEM((block_units, sub, wide), f32),
            pltpu.VMEM((block_rows, cols), bf16),
            pltpu.VMEM((block_rows, cols), bf16),
            pltpu.VMEM((block_rows, LANES), f32),
            pltpu.VMEM((block_rows, LANES), bf16),
            pltpu.VMEM((g1, 1, cols), f32),
            pltpu.VMEM((R, rank_rows, block_rows), bf16),
            pltpu.VMEM((rank_rows, cols), f32),
            pltpu.VMEM((rank_rows, cols), f32),
            pltpu.VMEM((g1, rank_rows, max(LANES, cols // g1)), f32),
            pltpu.VMEM((rank_rows, features), f32),
            pltpu.VMEM((g2, rank_rows, max(LANES, features // g2)), f32),
            dma((2,)),
            dma((2, units)),
            dma((units,)),
            dma((units,)),
            dma((units,)),
            dma((R // 2, block_units)),
            dma((R,)),
            dma((R,)),
            dma((g1,)),
            dma((g1,)),
            dma((R,)),
            dma((R,)),
        ] + [dma((g1,))] * 4 + [dma((g2,))] * 4,
        compiler_params=pltpu.CompilerParams(
            collective_id=0, has_side_effects=True, vmem_limit_bytes=VMEM_LIMIT
        ),
    )(
        tokens.reshape(S, sub, features), frozen_weight, input_adapter_factor,
        output_adapter_factor, magnitude.reshape(1, cols), cotangent, sequence_lengths,
    )
    return projected, grad_mag.reshape(cols), factor_grad, grad_b


def solution(mesh):
    in_specs = (
        P(("dp", "col"), "row"),
        P("row", "col"),
        P(None, "row"),
        P(None, "col"),
        P("col"),
        P(("dp", "row"), "col"),
        P("dp", None),
    )
    out_specs = (P(("dp", "row"), "col"), P("col"), P(None, "row"), P(None, "col"))
    return jax.shard_map(
        per_device, mesh=mesh, in_specs=in_specs, out_specs=out_specs, check_vma=False
    )
```

profile of v0, /device:TPU:0, one launch (start us, length us, event | category | flops | bytes accessed | tf_op | source)
XLA Modules:
  0.0 113.0 jit_solution(8170428634691261099)
XLA Ops:
  0.6 105.6 %shard_map.102 = (bf16[256,2048]{1,0:T(8,128)(2,1)}, f32[1,2048]{1,0:T(1,128)}, f32[16,2048]{1,0:T(8,128)}, f32[16,2048]{1,0:T(8,128)}) custom-call(bf16[4,64,2048]{2,1,0:T(8,128)(2,1)} %bitcast.3, bf16[2048,2048]{1,0:T(8,128)(2,1)} %w_hbm.1, bf16[16,2048]{1,0:T(8,128)(2,1)} %a_ref.1, bf16[16,2048]{1,0:T(8,128)(2,1)} %b_ref.1, f32[1,2048]{1,0:T(1,128)} %bitcast.4, ...), custom_call_target="tpu_custom_call" | custom-call | tf_op jit(solution)/shard_map/pallas_call | solution.py:439
  106.2 2.3 %copy.15 = bf16[256,2048]{1,0:T(8,128)(2,1)} copy(bf16[256,2048]{1,0:T(8,128)(2,1)} %get-tuple-element.16) | data formatting | bytes 2097152
  108.6 1.3 %copy.16 = f32[2048]{0:T(1024)} copy(f32[2048]{0:T(1024)} %bitcast.5) | data formatting | bytes 16384
  109.8 1.6 %copy.17 = f32[16,2048]{1,0:T(8,128)} copy(f32[16,2048]{1,0:T(8,128)} %get-tuple-element.18) | data formatting | bytes 262144
  111.4 1.6 %copy.18 = f32[16,2048]{1,0:T(8,128)} copy(f32[16,2048]{1,0:T(8,128)} %get-tuple-element.19) | data formatting | bytes 262144
where the time goes:
time: 113 us
  Pallas kernels  106 us (94%)
  local copies, waits for them, and re-layouts  6.73 us (6%)
    pallas_call x1, Pallas kernels, per_device(): pl.pallas_call(functools.partial(adapter_kernel, D, C, R, S), out_shape=(...  106 us
    unnamed x4, local copies, waits for them, and re-layouts  6.73 us

commit v1 on v0

v1 whole, which is shorter than its diff:
```python
import functools

import jax
import jax.numpy as jnp
from jax import lax
from jax.experimental import pallas as pl
from jax.experimental.pallas import tpu as pltpu
from jax.sharding import PartitionSpec as P

norm_eps = 1e-06
highest_precision = lax.Precision.HIGHEST
MESH = pl.DeviceIdType.MESH
LANES = 128
FEATURE_TILE = 512
VMEM_LIMIT = 56 * 1024 * 1024


def contract_product(left, right, left_dim, right_dim):
    return lax.dot_general(
        left, right, (((left_dim,), (right_dim,)), ((), ())), preferred_element_type=jnp.float32
    )


def column_tiles(width, tile):
    return [(start, min(tile, width - start)) for start in range(0, width, tile)]


def adapter_kernel(
    D, C, R, S, L,
    tok, w_hbm, a_hbm, b_hbm, magnitude_hbm, cot_hbm, lengths,
    projected, grad_mag, factor_grad, grad_b,
    wx, gath, sb, pin, xin, pb, st_in, st_pair, a_ref, b_ref, magnitude, apad, bpad, acc, own_sum, pg, cot, late_cot,
    row_weight, late_weight, down_in, down_all, merged_factor, col_norm, col_scale, coefficient_scale,
    scale_in, back_in, back_rows, bsum, bsum_all, box1, fsum, fsum_in, message, line_in, line_out, end_out, end_in,
    load_sem, tok_sem, plane_sem, line_sem, gsend, grecv, ssend, precv, xrecv, stsend, strecv,
    dn_send, dn_recv, dz_send, dz_recv, late_send, late_recv, sc_send, sc_recv, bk_send, bk_recv,
    fs_send, fs_recv, ln_send, ln_recv, end_send, end_recv, r1a, r1b, r1c, r1d,
):
    z = lax.axis_index("col")
    r = lax.axis_index("row")
    d = lax.axis_index("dp")
    p, q = r // 2, r % 2
    pairs = R // 2
    sub, features = tok.shape[1], tok.shape[2]
    cols = w_hbm.shape[1]
    rank_rows = a_ref.shape[0]
    units = C * S
    block_units = units // R
    block_rows = block_units * sub
    chunks = block_units // S
    tiles = column_tiles(cols, 512)
    feature_tiles = column_tiles(features, FEATURE_TILE)
    f32, bf16 = jnp.float32, jnp.bfloat16
    half = units // 2
    catch_up = half + 3
    rate = 4

    g1 = D * R
    me1 = d * R + r

    def device1(i):
        peer = (me1 + i) % g1
        return {"dp": peer // R, "row": peer % R}

    def loop(n, body):
        def turn(i, carry):
            body(i)
            return carry

        lax.fori_loop(1, n, turn, 0)

    def remote(src, dst, send_sem, recv_sem, device):
        return pltpu.make_async_remote_copy(
            src_ref=src, dst_ref=dst, send_sem=send_sem, recv_sem=recv_sem,
            device_id=device, device_id_type=MESH,
        )

    def signal(sem, device):
        pl.semaphore_signal(sem, inc=1, device_id=device, device_id_type=MESH)

    def signal_line(sem):
        @pl.when(z > 0)
        def _():
            signal(sem, {"col": z - 1})

        @pl.when(z < C - 1)
        def _():
            signal(sem, {"col": z + 1})

    line_count = jnp.where(z > 0, 1, 0) + jnp.where(z < C - 1, 1, 0)

    barrier = pltpu.get_barrier_semaphore()
    signal_line(barrier)
    for i in range(1, R):
        signal(barrier, {"row": (r + i) % R})
    for i in range(1, D):
        signal(barrier, {"dp": (d + i) % D})

    def load_tok(s):
        return pltpu.make_async_copy(tok.at[s], gath.at[z * S + s], tok_sem.at[s])

    small_loads = [
        pltpu.make_async_copy(a_hbm, a_ref, load_sem.at[0]),
        pltpu.make_async_copy(b_hbm, b_ref, load_sem.at[1]),
        pltpu.make_async_copy(magnitude_hbm, magnitude, load_sem.at[2]),
    ]
    load_w = pltpu.make_async_copy(w_hbm, wx, load_sem.at[3])
    load_c = pltpu.make_async_copy(cot_hbm, cot, load_sem.at[4])
    for s in range(S):
        load_tok(s).start()
    for load in small_loads:
        load.start()
    load_w.start()
    load_c.start()

    pl.semaphore_wait(barrier, line_count + R - 1 + D - 1)

    def hop(u, direction):
        target = z - 1 if direction == 0 else z + 1
        return remote(gath.at[u], gath.at[u], gsend.at[direction, u], grecv.at[u], {"col": target})

    for s in range(S):
        load_tok(s).wait()

        @pl.when(z > 0)
        def _():
            hop(z * S + s, 0).start()

        @pl.when(z < C - 1)
        def _():
            hop(z * S + s, 1).start()

    for i in range(1, D):
        signal(plane_sem, {"dp": (d + i) % D})
    for load in small_loads:
        load.wait()

    def down_copy(i, piece):
        return remote(
            down_in.at[piece], down_in.at[piece], dn_send.at[i], dn_recv.at[i], {"row": (r + i) % R}
        )

    def spread_copy(i, piece):
        return remote(
            down_all.at[piece], down_all.at[piece], dz_send.at[i], dz_recv.at[i], {"col": (z + i) % C}
        )

    a = a_ref[...]
    own_tokens = gath[pl.ds(z * S, S)].reshape(S * sub, features)
    down_in[r] = contract_product(a, own_tokens, 1, 1)
    for i in range(1, R):
        down_copy(i, r).start()
    apad[...] = jnp.zeros_like(apad)
    bpad[...] = jnp.zeros_like(bpad)
    apad[0:rank_rows, :] = a
    bpad[0:rank_rows, :] = b_ref[...]
    if C > 2:
        signal_line(line_sem.at[0])

    far_chunk = jnp.where(z > C - 1 - z, 0, C - 1)
    late_first = far_chunk * S + S - L
    late_owner = late_first // block_units
    late_slot = late_first % block_units

    def weights_of(first, rows):
        position = first + lax.broadcasted_iota(jnp.int32, (rows, LANES), 0)
        weights = jnp.zeros((rows, LANES), f32)
        start_row = 0
        for i in range(lengths.shape[1]):
            length = lengths[0, i]
            end_row = start_row + length
            inverse = 1.0 / jnp.full((1, LANES), length, jnp.int32).astype(f32)
            weights = jnp.where((position >= start_row) & (position < end_row), inverse, weights)
            start_row = end_row
        return weights

    row_weight[...] = weights_of(r * block_rows, block_rows)
    late_weight[...] = weights_of(late_first * sub, L * sub)

    load_w.wait()

    gram = contract_product(a, a, 1, 1)
    for start, width in tiles:
        span = pl.ds(start, width)
        st_in[r, 0:rank_rows, span] = jnp.dot(
            a, wx[:, span], preferred_element_type=f32
        ) + jnp.dot(
            gram, b_ref[:, span].astype(f32),
            precision=highest_precision, preferred_element_type=f32,
        )
        st_in[r, rank_rows:rank_rows + 8, span] = jnp.zeros((8, width), f32)
    depth = 256

    def norm_step(i, carry):
        rows = pl.ds(pl.multiple_of(i * depth, depth), depth)
        for start, width in tiles:
            span = pl.ds(start, width)
            merged = wx[rows, span].astype(f32) + contract_product(apad[:, rows], bpad[:, span], 0, 0)
            st_in[r, rank_rows:rank_rows + 1, span] += jnp.sum(merged * merged, axis=0, keepdims=True)
        return carry

    lax.fori_loop(0, features // depth, norm_step, 0)

    partner = p * 2 + (1 - q)

    def stat_near():
        return remote(st_in.at[r], st_in.at[r], stsend.at[0], strecv.at[0], {"row": partner})

    def stat_far(i, piece):
        return remote(
            st_pair.at[piece], st_pair.at[piece], stsend.at[i], strecv.at[i],
            {"row": ((p + i) % pairs) * 2 + q},
        )

    stat_near().start()

    def pair_stats():
        remote(st_in.at[partner], st_in.at[partner], stsend.at[0], strecv.at[0], {"row": partner}).wait_recv()
        st_pair[p] = st_in[r] + st_in[partner]
        for i in range(1, pairs):
            stat_far(i, p).start()

    def greet():
        pl.semaphore_wait(line_sem.at[0], line_count)
        for i in range(1, C - 2):
            signal_line(line_sem.at[i])
            if i < C - 3:
                pl.semaphore_wait(line_sem.at[i], line_count)

    def spread_down():
        if C > 3:
            pl.semaphore_wait(line_sem.at[C - 3], line_count)
        for i in range(1, R):
            down_copy(i, (r - i + R) % R).wait_recv()
        down = down_in[0]
        for i in range(1, R):
            down = down + down_in[i]
        down_all[z] = down.astype(bf16)
        loop(C, lambda i: spread_copy(i, z).start())

    near = jnp.minimum(z, C - 1 - z)

    def place(k):
        j = k - S
        both = j < 2 * near * S
        rest = j - 2 * near * S
        distance = jnp.where(both, j // (2 * S) + 1, near + 1 + rest // S)
        s = jnp.where(both, (j % (2 * S)) // 2, rest % S)
        leftward = jnp.where(both, j % 2 == 0, z > C - 1 - z)
        chunk = jnp.where(leftward, z - distance, z + distance)
        own = k < S
        return jnp.where(own, z, chunk), jnp.where(own, k, s)

    def unit_of(k):
        c, s = place(k)
        return c * S + s

    def pair_copy(u):
        return remote(sb.at[u], pin.at[u], ssend.at[u], precv.at[u], {"row": p * 2 + (1 - q)})

    def far_copy(u, owner_pair):
        return remote(
            sb.at[u], xin.at[p, u % block_units], ssend.at[u], xrecv.at[p, u % block_units],
            {"row": owner_pair * 2 + q},
        )

    late_pair, late_core = late_owner // 2, late_owner % 2

    def late_far(i):
        rows = pl.ds(pl.multiple_of(late_slot * sub, sub), L * sub)
        return remote(cot.at[rows], late_cot, late_send.at[i], late_recv, {"row": ((p + i) % pairs) * 2 + q})

    def late_near():
        return remote(late_cot, late_cot, late_send.at[0], late_recv, {"row": partner})

    def back_copy(i, piece):
        return remote(back_in.at[piece], back_in.at[piece], bk_send.at[i], bk_recv.at[i], {"row": (r + i) % R})

    def scale_copy(i, piece):
        return remote(scale_in.at[piece], scale_in.at[piece], sc_send.at[i], sc_recv.at[i], device1(i))

    def group_sum(g, me, device, src, box, out, s1, r1, s2, r2):
        width = max(LANES, src.shape[1] // g)
        pieces = src.shape[1] // width

        def part(j):
            return pl.ds(pl.multiple_of(j * width, width), width)

        def scatter(i):
            return remote(src.at[:, part((me + i) % g % pieces)], box.at[i], s1.at[i], r1.at[i], device(i))

        def spread(i, j):
            return remote(out.at[:, part(j % pieces)], out.at[:, part(j % pieces)], s2.at[i], r2.at[i], device(i))

        def to_owner(i, action):
            @pl.when((me + i) % g < pieces)
            def _():
                action(scatter(i))

        def from_owner(i, action):
            @pl.when((me - i + g) % g < pieces)
            def _():
                action(spread(i, (me - i + g) % g))

        def begin():
            loop(g, lambda i: to_owner(i, lambda copy: copy.start()))

        def middle():
            @pl.when(me < pieces)
            def _():
                def add(i, total):
                    scatter(i).wait_recv()
                    return total + box[i]

                out[:, part(me % pieces)] = lax.fori_loop(1, g, add, src[:, part(me % pieces)])
                loop(g, lambda i: spread(i, me).start())

        def end():
            loop(g, lambda i: from_owner(i, lambda copy: copy.wait_recv()))

        def drain():
            loop(g, lambda i: to_owner(i, lambda copy: copy.wait_send()))

            @pl.when(me < pieces)
            def _():
                loop(g, lambda i: spread(i, me).wait_send())

        return begin, middle, end, drain

    begin1, middle1, end1, drain1 = group_sum(
        g1, me1, device1, bsum, box1, bsum_all, r1a, r1b, r1c, r1d
    )

    def early():
        for i in range(1, pairs):
            stat_far(i, (p - i + pairs) % pairs).wait_recv()
        stats = st_pair[0]
        for i in range(1, pairs):
            stats = stats + st_pair[i]
        merged_factor[...] = stats[0:rank_rows]
        norm = jnp.sqrt(stats[rank_rows:rank_rows + 1] + norm_eps)
        col_norm[...] = norm
        col_scale[...] = magnitude[...] / norm
        coefficient_scale[...] = -magnitude[...] / (norm * norm * norm)
        load_c.wait()
        scale_in[me1] = jnp.zeros((1, cols), f32)
        for v in range(block_units):
            rows = pl.ds(v * sub, sub)
            weight = row_weight[rows, 0:1]
            for start, width in tiles:
                span = pl.ds(start, width)
                grad_out = cot[rows, span].astype(f32) * weight
                pg[rows, span] = (grad_out * col_scale[:, span]).astype(bf16)
        back_in[r] = contract_product(b_ref[...], pg[...], 1, 1).astype(bf16)
        for i in range(1, R):
            back_copy(i, r).start()

    def middle():
        loop(C, lambda i: spread_copy(i, (z - i + C) % C).wait_recv())
        for start, width in tiles:
            span = pl.ds(start, width)
            total = jnp.zeros((rank_rows, width), f32)
            for i in range(chunks):
                down = down_all[r * chunks + i]
                total = total + jnp.dot(
                    down, pg[i * S * sub:(i + 1) * S * sub, span], preferred_element_type=f32
                )
                acc[i * S:(i + 1) * S, :, span] = contract_product(
                    down, b_ref[:, span], 0, 0
                ).reshape(S, sub, width)
            bsum[:, span] = total
        if D > 1:
            pl.semaphore_wait(plane_sem, D - 1)
        begin1()

        @pl.when(r == late_owner)
        def _():
            for i in range(L):
                rows = pl.ds(pl.multiple_of((late_slot + i) * sub, sub), sub)
                weight = row_weight[rows, 0:1]
                for start, width in tiles:
                    span = pl.ds(start, width)
                    grad_out = cot[rows, span].astype(f32) * weight
                    scale_in[me1, :, span] += jnp.sum(
                        grad_out * acc[late_slot + i, :, span], axis=0, keepdims=True
                    )

    def send_late():
        @pl.when(r == late_owner)
        def _():
            for i in range(1, pairs):
                late_far(i).start()
            late_cot[...] = cot[pl.ds(pl.multiple_of(late_slot * sub, sub), L * sub), :]

    def pass_late():
        @pl.when(q == late_core)
        def _():
            @pl.when(p != late_pair)
            def _():
                late_near().wait_recv()

            late_near().start()

    def multiply(k):
        c, s = place(k)
        u = c * S + s
        owner = u // block_units

        @pl.when(k >= S)
        def _():
            hop(u, 0).wait_recv()

            @pl.when((c < z) & (z < C - 1))
            def _():
                hop(u, 1).start()

            @pl.when((c > z) & (z > 0))
            def _():
                hop(u, 0).start()

        slot = k % 2
        for start, width in tiles:
            span = pl.ds(start, width)
            pb[slot, :, span] = jnp.dot(gath[u], wx[:, span], preferred_element_type=f32)

        @pl.when(k >= units - L)
        def _():
            @pl.when((k == units - L) & (q != late_core))
            def _():
                late_near().wait_recv()

            rows = pl.ds(pl.multiple_of((k - units + L) * sub, sub), sub)
            weight = late_weight[rows, 0:1]
            for start, width in tiles:
                span = pl.ds(start, width)
                grad_out = late_cot[rows, span].astype(f32) * weight
                scale_in[me1, :, span] += jnp.sum(grad_out * pb[slot, :, span], axis=0, keepdims=True)

        @pl.when(k == units - 1)
        def _():
            loop(g1, lambda i: scale_copy(i, me1).start())

        @pl.when(owner % 2 != q)
        def _():
            sb[u] = pb[slot].astype(bf16)
            pair_copy(u).start()

    def combine(k):
        u = unit_of(k)
        owner = u // block_units
        slot = k % 2

        @pl.when(owner % 2 == q)
        def _():
            pair_copy(u).wait_recv()
            total = pb[slot] + pin[u].astype(f32)

            @pl.when(owner // 2 == p)
            def _():
                own_sum[u % block_units] = total

            @pl.when(owner // 2 != p)
            def _():
                sb[u] = total.astype(bf16)
                far_copy(u, owner // 2).start()

    def factor_term(k):
        u = unit_of(k)
        block = u // block_units
        rows = pl.ds(pl.multiple_of((u % block_units) * sub, sub), sub)
        back = back_rows[block, rows, :]
        for start, width in feature_tiles:
            span = pl.ds(start, width)
            fsum[:, span] += contract_product(back, gath[u, :, span], 0, 0)[0:rank_rows]

    def finish(k):
        u = unit_of(k)

        @pl.when(u // block_units == r)
        def _():
            v = u % block_units
            for i in range(1, pairs):
                other = (p + i) % pairs
                remote(
                    sb.at[v], xin.at[other, v], ssend.at[v], xrecv.at[other, v], {"row": other * 2 + q}
                ).wait_recv()
            rows = pl.ds(pl.multiple_of(v * sub, sub), sub)
            weight = row_weight[rows, 0:1]
            for start, width in tiles:
                span = pl.ds(start, width)
                query = acc[v, :, span] + own_sum[v, :, span]
                for i in range(1, pairs):
                    query = query + xin[(p + i) % pairs, v, :, span].astype(f32)
                projected[rows, span] = (query * col_scale[:, span]).astype(bf16)
                grad_out = cot[rows, span].astype(f32) * weight

                @pl.when(k < units - L)
                def _():
                    scale_in[me1, :, span] += jnp.sum(grad_out * query, axis=0, keepdims=True)

    def each(first, last, body):
        def turn(i, carry):
            body(i)
            return carry

        lax.fori_loop(first, last, turn, 0)

    fsum[...] = jnp.zeros_like(fsum)

    def step(k, carry):
        @pl.when(k > 0)
        def _():
            combine(k - 1)

        @pl.when(k == 1)
        def _():
            pair_stats()

        if C > 2:
            @pl.when(k == 2)
            def _():
                greet()

        @pl.when(k == S)
        def _():
            spread_down()

        @pl.when(k == half)
        def _():
            early()

        @pl.when(k == half + 1)
        def _():
            send_late()

        @pl.when(k == half + 2)
        def _():
            middle()

        @pl.when(k == catch_up)
        def _():
            for i in range(1, R):
                back_copy(i, (r - i + R) % R).wait_recv()
            one = (
                lax.broadcasted_iota(jnp.int32, (rank_rows, LANES), 0)
                == lax.broadcasted_iota(jnp.int32, (rank_rows, LANES), 1)
            ).astype(f32).astype(bf16)
            for j in range(R):
                back_rows[j] = contract_product(back_in[j], one, 0, 0).astype(bf16)

        @pl.when(k >= catch_up)
        def _():
            done = rate * (k - catch_up)
            each(jnp.minimum(done, k - 1), jnp.minimum(done + rate, k), factor_term)
            each(jnp.minimum(done, k - 2), jnp.minimum(done + rate, k - 1), finish)

        @pl.when(k == catch_up + 1)
        def _():
            pass_late()

        @pl.when(k == units - 2)
        def _():
            middle1()

        multiply(k)
        return carry

    lax.fori_loop(0, units, step, 0)

    factor_term(units - 1)

    def group_copy(i, piece):
        return remote(fsum_in.at[piece], fsum_in.at[piece], fs_send.at[i], fs_recv.at[i], {"dp": (d + i) % D})

    fsum_in[d] = fsum[...].astype(bf16)
    for i in range(1, D):
        group_copy(i, d).start()
    combine(units - 1)

    ends = (z == 0) | (z == C - 1)
    side = jnp.where(z == 0, 0, 1)

    def end_copy(i, t):
        target = jnp.where(z == 0, i, C - 1 - i)
        return remote(end_out.at[t], end_in.at[side, t], end_send.at[i, t], end_recv.at[side, t], {"col": target})

    def end_arrived(j):
        for t, (start, width) in enumerate(feature_tiles):
            span = pl.ds(start, width)
            remote(
                end_out.at[t], end_in.at[j, t], end_send.at[0, t], end_recv.at[j, t], {"col": (z + 1) % C}
            ).wait_recv()
            message[:, span] += end_in[j, t].astype(f32)

    def line_copy(direction):
        target = z - 1 if direction == 0 else z + 1
        return remote(
            line_out.at[direction], line_in.at[direction], ln_send.at[direction], ln_recv.at[direction],
            {"col": target},
        )

    loop(g1, lambda i: scale_copy(i, (me1 - i + g1) % g1).wait_recv())
    scale_grad = scale_in[0]
    for j in range(1, g1):
        scale_grad = scale_grad + scale_in[j]
    coefficient = scale_grad * coefficient_scale[...]
    scaled = (b_ref[...].astype(f32) * coefficient).astype(bf16)
    cross = contract_product(scaled, b_ref[...], 1, 1)
    for t, (start, width) in enumerate(feature_tiles):
        span = pl.ds(start, width)
        total = contract_product(scaled, wx[span, :], 1, 1) + jnp.dot(
            cross, a_ref[:, span].astype(f32),
            precision=highest_precision, preferred_element_type=f32,
        )
        total = total + fsum[:, span]
        if t == 0:
            for i in range(1, D):
                group_copy(i, (d - i + D) % D).wait_recv()
        for i in range(1, D):
            total = total + fsum_in[(d - i + D) % D, :, span].astype(f32)
        message[:, span] = total

        @pl.when(ends)
        def _():
            end_out[t] = message[:, span].astype(bf16)
            for i in range(C - 1, 0, -1):
                end_copy(i, t).start()

    if C > 2:
        @pl.when((z > 0) & (z < C - 1))
        def _():
            own = message[...]
            for direction in (0, 1):
                more = (z < C - 2) if direction == 0 else (z > 1)

                @pl.when(more)
                def _():
                    line_copy(direction).wait_recv()
                    incoming = line_in[direction].astype(f32)
                    line_out[direction] = (own + incoming).astype(bf16)
                    message[...] += incoming

                @pl.when(jnp.logical_not(more))
                def _():
                    line_out[direction] = own.astype(bf16)

                line_copy(direction).start()

    each(units - 2, units, finish)
    grad_mag[...] = scale_grad / col_norm[...]
    end1()
    grad_b[...] = bsum_all[...] + merged_factor[...] * coefficient

    drain1()
    loop(g1, lambda i: scale_copy(i, me1).wait_send())
    for i in range(1, R):
        back_copy(i, r).wait_send()
        down_copy(i, r).wait_send()
    loop(C, lambda i: spread_copy(i, z).wait_send())
    for i in range(1, D):
        group_copy(i, d).wait_send()

    stat_near().wait_send()
    for i in range(1, pairs):
        stat_far(i, p).wait_send()

    @pl.when(r == late_owner)
    def _():
        for i in range(1, pairs):
            late_far(i).wait_send()

    @pl.when(q == late_core)
    def _():
        late_near().wait_send()

    def drain(u, carry):
        c = u // S
        owner = u // block_units

        @pl.when((owner % 2 != q) | (owner // 2 != p))
        def _():
            pair_copy(u).wait_send()

        @pl.when((c <= z) & (z < C - 1))
        def _():
            hop(u, 1).wait_send()

        @pl.when((c >= z) & (z > 0))
        def _():
            hop(u, 0).wait_send()

        return carry

    lax.fori_loop(0, units, drain, 0)

    if C > 2:
        @pl.when(z == 0)
        def _():
            line_copy(0).wait_recv()
            message[...] += line_in[0].astype(f32)

        @pl.when(z == C - 1)
        def _():
            line_copy(1).wait_recv()
            message[...] += line_in[1].astype(f32)

    @pl.when(z > 0)
    def _():
        end_arrived(0)

    @pl.when(z < C - 1)
    def _():
        end_arrived(1)

    factor_grad[...] = message[...]

    @pl.when(ends)
    def _():
        for t in range(len(feature_tiles)):
            for i in range(C - 1, 0, -1):
                end_copy(i, t).wait_send()

    if C > 2:
        @pl.when((z > 0) & (z < C - 1))
        def _():
            line_copy(0).wait_send()
            line_copy(1).wait_send()


def per_device(
    tokens,
    frozen_weight,
    input_adapter_factor,
    output_adapter_factor,
    magnitude,
    cotangent,
    sequence_lengths,
):
    D, C, R = lax.axis_size("dp"), lax.axis_size("col"), lax.axis_size("row")
    local_rows, features = tokens.shape
    block_rows, cols = cotangent.shape
    rank_rows = input_adapter_factor.shape[0]
    S, L = 4, 2
    feature_tiles = features // FEATURE_TILE
    sub = local_rows // S
    units = C * S
    block_units = units // R
    g1 = D * R
    vmem = pl.BlockSpec(memory_space=pltpu.VMEM)
    smem = pl.BlockSpec(memory_space=pltpu.SMEM)
    hbm = pl.BlockSpec(memory_space=pl.ANY)
    dma = pltpu.SemaphoreType.DMA
    regular = pltpu.SemaphoreType.REGULAR
    f32, bf16 = jnp.float32, jnp.bfloat16
    projected, grad_mag, factor_grad, grad_b = pl.pallas_call(
        functools.partial(adapter_kernel, D, C, R, S, L),
        out_shape=(
            pltpu.VMEM((block_rows, cols), bf16),
            pltpu.VMEM((1, cols), f32),
            pltpu.VMEM((rank_rows, features), f32),
            pltpu.VMEM((rank_rows, cols), f32),
        ),
        in_specs=[hbm, hbm, hbm, hbm, hbm, hbm, smem],
        out_specs=(vmem, vmem, vmem, vmem),
        scratch_shapes=[
            pltpu.VMEM((features, cols), bf16),
            pltpu.VMEM((units, sub, features), bf16),
            pltpu.VMEM((units, sub, cols), bf16),
            pltpu.VMEM((units, sub, cols), bf16),
            pltpu.VMEM((R // 2, block_units, sub, cols), bf16),
            pltpu.VMEM((2, sub, cols), f32),
            pltpu.VMEM((R, rank_rows + 8, cols), f32),
            pltpu.VMEM((R // 2, rank_rows + 8, cols), f32),
            pltpu.VMEM((rank_rows, features), bf16),
            pltpu.VMEM((rank_rows, cols), bf16),
            pltpu.VMEM((1, cols), f32),
            pltpu.VMEM((LANES, features), bf16),
            pltpu.VMEM((LANES, cols), bf16),
            pltpu.VMEM((block_units, sub, cols), f32),
            pltpu.VMEM((block_units, sub, cols), f32),
            pltpu.VMEM((block_rows, cols), bf16),
            pltpu.VMEM((block_rows, cols), bf16),
            pltpu.VMEM((L * sub, cols), bf16),
            pltpu.VMEM((block_rows, LANES), f32),
            pltpu.VMEM((L * sub, LANES), f32),
            pltpu.VMEM((R, rank_rows, local_rows), f32),
            pltpu.VMEM((C, rank_rows, local_rows), bf16),
            pltpu.VMEM((rank_rows, cols), f32),
            pltpu.VMEM((1, cols), f32),
            pltpu.VMEM((1, cols), f32),
            pltpu.VMEM((1, cols), f32),
            pltpu.VMEM((g1, 1, cols), f32),
            pltpu.VMEM((R, rank_rows, block_rows), bf16),
            pltpu.VMEM((R, block_rows, LANES), bf16),
            pltpu.VMEM((rank_rows, cols), f32),
            pltpu.VMEM((rank_rows, cols), f32),
            pltpu.VMEM((g1, rank_rows, max(LANES, cols // g1)), f32),
            pltpu.VMEM((rank_rows, features), f32),
            pltpu.VMEM((D, rank_rows, features), bf16),
            pltpu.VMEM((rank_rows, features), f32),
            pltpu.VMEM((2, rank_rows, features), bf16),
            pltpu.VMEM((2, rank_rows, features), bf16),
            pltpu.VMEM((feature_tiles, rank_rows, features // feature_tiles), bf16),
            pltpu.VMEM((2, feature_tiles, rank_rows, features // feature_tiles), bf16),
            dma((5,)),
            dma((S,)),
            regular,
            pltpu.SemaphoreType.REGULAR((max(1, C - 2),)),
            dma((2, units)),
            dma((units,)),
            dma((units,)),
            dma((units,)),
            dma((R // 2, block_units)),
            dma((R,)),
            dma((R,)),
            dma((R,)),
            dma((R,)),
            dma((C,)),
            dma((C,)),
            dma((R,)),
            dma(()),
            dma((g1,)),
            dma((g1,)),
            dma((R,)),
            dma((R,)),
            dma((D,)),
            dma((D,)),
            dma((2,)),
            dma((2,)),
            dma((C, feature_tiles)),
            dma((2, feature_tiles)),
        ] + [dma((g1,))] * 4,
        compiler_params=pltpu.CompilerParams(
            collective_id=0, has_side_effects=True, vmem_limit_bytes=VMEM_LIMIT
        ),
    )(
        tokens.reshape(S, sub, features), frozen_weight, input_adapter_factor,
        output_adapter_factor, magnitude.reshape(1, cols), cotangent, sequence_lengths,
    )
    return projected, grad_mag.reshape(cols), factor_grad, grad_b


def solution(mesh):
    in_specs = (
        P(("dp", "col"), "row"),
        P("row", "col"),
        P(None, "row"),
        P(None, "col"),
        P("col"),
        P(("dp", "row"), "col"),
        P("dp", None),
    )
    out_specs = (P(("dp", "row"), "col"), P("col"), P(None, "row"), P(None, "col"))
    return jax.shard_map(
        per_device, mesh=mesh, in_specs=in_specs, out_specs=out_specs, check_vma=False
    )
```

time: 113 us -> 93.4 us (0.83)
  Pallas kernels: 106 us -> 89.7 us
  local copies, waits for them, and re-layouts: 6.73 us -> 2.88 us
    pallas_call x1, Pallas kernels: 106 us -> 89.7 us  [per_device(): pl.pallas_call(functools.partial(adapter_kernel, D, C, R, S, L), out_shap...]
    unnamed x4, local copies, waits for them, and re-layouts: 6.73 us -> 2.88 us
where the time goes in v1:
time: 93.4 us; the launch traced here: 93.2 us
  Pallas kernels  89.7 us (96%)
  local copies, waits for them, and re-layouts  2.88 us (3%)
    pallas_call x1, Pallas kernels, per_device(): pl.pallas_call(functools.partial(adapter_kernel, D, C, R, S, L), out_shap...  89.7 us
    unnamed x4, local copies, waits for them, and re-layouts  2.88 us

profile of v1, /device:TPU:0, one launch (start us, length us, event | category | flops | bytes accessed | tf_op | source)
XLA Modules:
  0.0 93.2 jit_solution(16677696560842713056)
XLA Ops:
  0.6 89.7 %shard_map.102 = (bf16[256,2048]{1,0:T(8,128)(2,1)S(1)}, f32[1,2048]{1,0:T(1,128)S(1)}, f32[16,2048]{1,0:T(8,128)S(1)}, f32[16,2048]{1,0:T(8,128)S(1)}) custom-call(bf16[4,64,2048]{2,1,0:T(8,128)(2,1)} %bitcast.4, bf16[2048,2048]{1,0:T(8,128)(2,1)} %w_hbm.1, bf16[16,2048]{1,0:T(8,128)(2,1)} %a_hbm.1, bf16[16,2048]{1,0:T(8,128)(2,1)} %b_hbm.1, ...), custom_call_target="tpu_custom_call" | custom-call | tf_op jit(solution)/shard_map/pallas_call | solution.py:755
  90.3 1.0 %copy.15 = bf16[256,2048]{1,0:T(8,128)(2,1)} copy(bf16[256,2048]{1,0:T(8,128)(2,1)S(1)} %get-tuple-element.12) | data formatting | bytes 2097152
  91.3 0.6 copy.16
  91.9 0.7 copy.17
  92.5 0.7 copy.18

commit v2 on v1

--- a/solution.py
+++ b/solution.py
@@ -27,9 +27,9 @@
 
 def adapter_kernel(
     D, C, R, S, L,
-    tok, w_hbm, a_hbm, b_hbm, magnitude_hbm, cot_hbm, lengths,
+    tok, w_hbm, a_hbm, b_hbm, magnitude_hbm, cot_hbm, lengths_hbm,
     projected, grad_mag, factor_grad, grad_b,
-    wx, gath, sb, pin, xin, pb, st_in, st_pair, a_ref, b_ref, magnitude, apad, bpad, acc, own_sum, pg, cot, late_cot,
+    lengths, wx, gath, sb, pin, xin, pb, st_in, st_pair, a_ref, b_ref, magnitude, apad, bpad, acc, own_sum, pg, cot, late_cot,
     row_weight, late_weight, down_in, down_all, merged_factor, col_norm, col_scale, coefficient_scale,
     scale_in, back_in, back_rows, bsum, bsum_all, box1, fsum, fsum_in, message, line_in, line_out, end_out, end_in,
     load_sem, tok_sem, plane_sem, line_sem, gsend, grecv, ssend, precv, xrecv, stsend, strecv,
@@ -75,6 +75,9 @@
             device_id=device, device_id_type=MESH,
         )
 
+    def settle(view, sem, device):
+        return remote(view, view, sem, sem, device)
+
     def signal(sem, device):
         pl.semaphore_signal(sem, inc=1, device_id=device, device_id_type=MESH)
 
@@ -103,6 +106,7 @@
         pltpu.make_async_copy(a_hbm, a_ref, load_sem.at[0]),
         pltpu.make_async_copy(b_hbm, b_ref, load_sem.at[1]),
         pltpu.make_async_copy(magnitude_hbm, magnitude, load_sem.at[2]),
+        pltpu.make_async_copy(lengths_hbm, lengths, load_sem.at[5]),
     ]
     load_w = pltpu.make_async_copy(w_hbm, wx, load_sem.at[3])
     load_c = pltpu.make_async_copy(cot_hbm, cot, load_sem.at[4])
@@ -117,7 +121,8 @@
 
     def hop(u, direction):
         target = z - 1 if direction == 0 else z + 1
-        return remote(gath.at[u], gath.at[u], gsend.at[direction, u], grecv.at[u], {"col": target})
+        slot = u if direction == 0 else jnp.where(u // S == z, units + u % S, u)
+        return remote(gath.at[u], gath.at[u], gsend.at[slot], grecv.at[u], {"col": target})
 
     for s in range(S):
         load_tok(s).wait()
@@ -137,12 +142,12 @@
 
     def down_copy(i, piece):
         return remote(
-            down_in.at[piece], down_in.at[piece], dn_send.at[i], dn_recv.at[i], {"row": (r + i) % R}
+            down_in.at[piece], down_in.at[piece], dn_send, dn_recv, {"row": (r + i) % R}
         )
 
     def spread_copy(i, piece):
         return remote(
-            down_all.at[piece], down_all.at[piece], dz_send.at[i], dz_recv.at[i], {"col": (z + i) % C}
+            down_all.at[piece], down_all.at[piece], dz_send, dz_recv, {"col": (z + i) % C}
         )
 
     a = a_ref[...]
@@ -208,7 +213,7 @@
 
     def stat_far(i, piece):
         return remote(
-            st_pair.at[piece], st_pair.at[piece], stsend.at[i], strecv.at[i],
+            st_pair.at[piece], st_pair.at[piece], stsend.at[1], strecv.at[1],
             {"row": ((p + i) % pairs) * 2 + q},
         )
 
@@ -230,8 +235,7 @@
     def spread_down():
         if C > 3:
             pl.semaphore_wait(line_sem.at[C - 3], line_count)
-        for i in range(1, R):
-            down_copy(i, (r - i + R) % R).wait_recv()
+        settle(down_in.at[pl.ds(0, R - 1)], dn_recv, {"row": partner}).wait_recv()
         down = down_in[0]
         for i in range(1, R):
             down = down + down_in[i]
@@ -256,11 +260,13 @@
         return c * S + s
 
     def pair_copy(u):
-        return remote(sb.at[u], pin.at[u], ssend.at[u], precv.at[u], {"row": p * 2 + (1 - q)})
+        slot = u // block_units // 2 * block_units + u % block_units
+        return remote(sb.at[u], pin.at[u], ssend.at[u], precv.at[slot], {"row": p * 2 + (1 - q)})
 
     def far_copy(u, owner_pair):
         return remote(
-            sb.at[u], xin.at[p, u % block_units], ssend.at[u], xrecv.at[p, u % block_units],
+            sb.at[u], xin.at[p, u % block_units], ssend.at[u],
+            xrecv.at[(p - owner_pair + pairs) % pairs - 1, u % block_units],
             {"row": owner_pair * 2 + q},
         )
 
@@ -274,10 +280,10 @@
         return remote(late_cot, late_cot, late_send.at[0], late_recv, {"row": partner})
 
     def back_copy(i, piece):
-        return remote(back_in.at[piece], back_in.at[piece], bk_send.at[i], bk_recv.at[i], {"row": (r + i) % R})
+        return remote(back_in.at[piece], back_in.at[piece], bk_send, bk_recv, {"row": (r + i) % R})
 
     def scale_copy(i, piece):
-        return remote(scale_in.at[piece], scale_in.at[piece], sc_send.at[i], sc_recv.at[i], device1(i))
+        return remote(scale_in.at[piece], scale_in.at[piece], sc_send, sc_recv, device1(i))
 
     def group_sum(g, me, device, src, box, out, s1, r1, s2, r2):
         width = max(LANES, src.shape[1] // g)
@@ -287,43 +293,54 @@
             return pl.ds(pl.multiple_of(j * width, width), width)
 
         def scatter(i):
-            return remote(src.at[:, part((me + i) % g % pieces)], box.at[i], s1.at[i], r1.at[i], device(i))
+            return remote(src.at[:, part((me + i) % g % pieces)], box.at[i], s1, r1, device(i))
 
         def spread(i, j):
-            return remote(out.at[:, part(j % pieces)], out.at[:, part(j % pieces)], s2.at[i], r2.at[i], device(i))
-
-        def to_owner(i, action):
-            @pl.when((me + i) % g < pieces)
-            def _():
-                action(scatter(i))
-
-        def from_owner(i, action):
-            @pl.when((me - i + g) % g < pieces)
-            def _():
-                action(spread(i, (me - i + g) % g))
+            return remote(out.at[:, part(j % pieces)], out.at[:, part(j % pieces)], s2, r2, device(i))
+
+        def await_pieces(count, sem, sent):
+            if count > 0:
+                copies = settle(box.at[pl.ds(0, count)], sem, device(1))
+                copies.wait_send() if sent else copies.wait_recv()
+
+        def await_owners(sem, sent):
+            if pieces == g:
+                await_pieces(pieces - 1, sem, sent)
+            else:
+                @pl.when(me < pieces)
+                def _():
+                    await_pieces(pieces - 1, sem, sent)
+
+                @pl.when(me >= pieces)
+                def _():
+                    await_pieces(pieces, sem, sent)
 
         def begin():
-            loop(g, lambda i: to_owner(i, lambda copy: copy.start()))
+            def send(i):
+                @pl.when((me + i) % g < pieces)
+                def _():
+                    scatter(i).start()
+
+            loop(g, send)
 
         def middle():
             @pl.when(me < pieces)
             def _():
-                def add(i, total):
-                    scatter(i).wait_recv()
-                    return total + box[i]
-
-                out[:, part(me % pieces)] = lax.fori_loop(1, g, add, src[:, part(me % pieces)])
+                await_pieces(g - 1, r1, False)
+                out[:, part(me % pieces)] = lax.fori_loop(
+                    1, g, lambda i, total: total + box[i], src[:, part(me % pieces)]
+                )
                 loop(g, lambda i: spread(i, me).start())
 
         def end():
-            loop(g, lambda i: from_owner(i, lambda copy: copy.wait_recv()))
+            await_owners(r2, False)
 
         def drain():
-            loop(g, lambda i: to_owner(i, lambda copy: copy.wait_send()))
+            await_owners(s1, True)
 
             @pl.when(me < pieces)
             def _():
-                loop(g, lambda i: spread(i, me).wait_send())
+                await_pieces(g - 1, s2, True)
 
         return begin, middle, end, drain
 
@@ -332,8 +349,8 @@
     )
 
     def early():
-        for i in range(1, pairs):
-            stat_far(i, (p - i + pairs) % pairs).wait_recv()
+        if pairs > 1:
+            settle(st_pair.at[pl.ds(0, pairs - 1)], strecv.at[1], {"row": partner}).wait_recv()
         stats = st_pair[0]
         for i in range(1, pairs):
             stats = stats + st_pair[i]
@@ -356,7 +373,7 @@
             back_copy(i, r).start()
 
     def middle():
-        loop(C, lambda i: spread_copy(i, (z - i + C) % C).wait_recv())
+        settle(down_all.at[pl.ds(0, C - 1)], dz_recv, {"row": partner}).wait_recv()
         for start, width in tiles:
             span = pl.ds(start, width)
             total = jnp.zeros((rank_rows, width), f32)
@@ -482,7 +499,7 @@
             for i in range(1, pairs):
                 other = (p + i) % pairs
                 remote(
-                    sb.at[v], xin.at[other, v], ssend.at[v], xrecv.at[other, v], {"row": other * 2 + q}
+                    sb.at[v], xin.at[other, v], ssend.at[v], xrecv.at[i - 1, v], {"row": other * 2 + q}
                 ).wait_recv()
             rows = pl.ds(pl.multiple_of(v * sub, sub), sub)
             weight = row_weight[rows, 0:1]
@@ -539,8 +556,7 @@
 
         @pl.when(k == catch_up)
         def _():
-            for i in range(1, R):
-                back_copy(i, (r - i + R) % R).wait_recv()
+            settle(back_in.at[pl.ds(0, R - 1)], bk_recv, {"row": partner}).wait_recv()
             one = (
                 lax.broadcasted_iota(jnp.int32, (rank_rows, LANES), 0)
                 == lax.broadcasted_iota(jnp.int32, (rank_rows, LANES), 1)
@@ -570,7 +586,7 @@
     factor_term(units - 1)
 
     def group_copy(i, piece):
-        return remote(fsum_in.at[piece], fsum_in.at[piece], fs_send.at[i], fs_recv.at[i], {"dp": (d + i) % D})
+        return remote(fsum_in.at[piece], fsum_in.at[piece], fs_send, fs_recv, {"dp": (d + i) % D})
 
     fsum_in[d] = fsum[...].astype(bf16)
     for i in range(1, D):
@@ -582,15 +598,12 @@
 
     def end_copy(i, t):
         target = jnp.where(z == 0, i, C - 1 - i)
-        return remote(end_out.at[t], end_in.at[side, t], end_send.at[i, t], end_recv.at[side, t], {"col": target})
+        return remote(end_out.at[t], end_in.at[side, t], end_send.at[i], end_recv.at[side], {"col": target})
 
     def end_arrived(j):
+        settle(end_in.at[j], end_recv.at[j], {"row": partner}).wait_recv()
         for t, (start, width) in enumerate(feature_tiles):
-            span = pl.ds(start, width)
-            remote(
-                end_out.at[t], end_in.at[j, t], end_send.at[0, t], end_recv.at[j, t], {"col": (z + 1) % C}
-            ).wait_recv()
-            message[:, span] += end_in[j, t].astype(f32)
+            message[:, pl.ds(start, width)] += end_in[j, t].astype(f32)
 
     def line_copy(direction):
         target = z - 1 if direction == 0 else z + 1
@@ -599,7 +612,7 @@
             {"col": target},
         )
 
-    loop(g1, lambda i: scale_copy(i, (me1 - i + g1) % g1).wait_recv())
+    settle(scale_in.at[pl.ds(0, g1 - 1)], sc_recv, device1(1)).wait_recv()
     scale_grad = scale_in[0]
     for j in range(1, g1):
         scale_grad = scale_grad + scale_in[j]
@@ -613,9 +626,8 @@
             precision=highest_precision, preferred_element_type=f32,
         )
         total = total + fsum[:, span]
-        if t == 0:
-            for i in range(1, D):
-                group_copy(i, (d - i + D) % D).wait_recv()
+        if t == 0 and D > 1:
+            settle(fsum_in.at[pl.ds(0, D - 1)], fs_recv, {"row": partner}).wait_recv()
         for i in range(1, D):
             total = total + fsum_in[(d - i + D) % D, :, span].astype(f32)
         message[:, span] = total
@@ -623,8 +635,13 @@
         @pl.when(ends)
         def _():
             end_out[t] = message[:, span].astype(bf16)
-            for i in range(C - 1, 0, -1):
+            for i in range(C - 1, 1, -1):
                 end_copy(i, t).start()
+
+    @pl.when(ends)
+    def _():
+        for t in range(len(feature_tiles)):
+            end_copy(1, t).start()
 
     if C > 2:
         @pl.when((z > 0) & (z < C - 1))
@@ -652,17 +669,16 @@
     grad_b[...] = bsum_all[...] + merged_factor[...] * coefficient
 
     drain1()
-    loop(g1, lambda i: scale_copy(i, me1).wait_send())
-    for i in range(1, R):
-        back_copy(i, r).wait_send()
-        down_copy(i, r).wait_send()
-    loop(C, lambda i: spread_copy(i, z).wait_send())
-    for i in range(1, D):
-        group_copy(i, d).wait_send()
+    settle(scale_in.at[pl.ds(0, g1 - 1)], sc_send, device1(1)).wait_send()
+    settle(back_in.at[pl.ds(0, R - 1)], bk_send, {"row": partner}).wait_send()
+    settle(down_in.at[pl.ds(0, R - 1)], dn_send, {"row": partner}).wait_send()
+    settle(down_all.at[pl.ds(0, C - 1)], dz_send, {"row": partner}).wait_send()
+    if D > 1:
+        settle(fsum_in.at[pl.ds(0, D - 1)], fs_send, {"row": partner}).wait_send()
 
     stat_near().wait_send()
-    for i in range(1, pairs):
-        stat_far(i, p).wait_send()
+    if pairs > 1:
+        settle(st_pair.at[pl.ds(0, pairs - 1)], stsend.at[1], {"row": partner}).wait_send()
 
     @pl.when(r == late_owner)
     def _():
@@ -716,15 +732,24 @@
 
     @pl.when(ends)
     def _():
-        for t in range(len(feature_tiles)):
-            for i in range(C - 1, 0, -1):
-                end_copy(i, t).wait_send()
+        for i in range(C - 1, 0, -1):
+            settle(end_out, end_send.at[i], {"row": partner}).wait_send()
 
     if C > 2:
         @pl.when((z > 0) & (z < C - 1))
         def _():
             line_copy(0).wait_send()
             line_copy(1).wait_send()
+
+
+def hand_over_kernel(*refs):
+    n = (len(refs) - 1) // 2
+    sources, targets, sems = refs[:n], refs[n:2 * n], refs[-1]
+    stores = [pltpu.make_async_copy(sources[i], targets[i], sems.at[i]) for i in range(n)]
+    for store in stores:
+        store.start()
+    for store in stores:
+        store.wait()
 
 
 def per_device(
@@ -747,12 +772,11 @@
     block_units = units // R
     g1 = D * R
     vmem = pl.BlockSpec(memory_space=pltpu.VMEM)
-    smem = pl.BlockSpec(memory_space=pltpu.SMEM)
     hbm = pl.BlockSpec(memory_space=pl.ANY)
     dma = pltpu.SemaphoreType.DMA
     regular = pltpu.SemaphoreType.REGULAR
     f32, bf16 = jnp.float32, jnp.bfloat16
-    projected, grad_mag, factor_grad, grad_b = pl.pallas_call(
+    results = pl.pallas_call(
         functools.partial(adapter_kernel, D, C, R, S, L),
         out_shape=(
             pltpu.VMEM((block_rows, cols), bf16),
@@ -760,9 +784,10 @@
             pltpu.VMEM((rank_rows, features), f32),
             pltpu.VMEM((rank_rows, cols), f32),
         ),
-        in_specs=[hbm, hbm, hbm, hbm, hbm, hbm, smem],
+        in_specs=[hbm] * 7,
         out_specs=(vmem, vmem, vmem, vmem),
         scratch_shapes=[
+            pltpu.SMEM(sequence_lengths.shape, jnp.int32),
             pltpu.VMEM((features, cols), bf16),
             pltpu.VMEM((units, sub, features), bf16),
             pltpu.VMEM((units, sub, cols), bf16),
@@ -802,34 +827,34 @@
             pltpu.VMEM((2, rank_rows, features), bf16),
             pltpu.VMEM((feature_tiles, rank_rows, features // feature_tiles), bf16),
             pltpu.VMEM((2, feature_tiles, rank_rows, features // feature_tiles), bf16),
-            dma((5,)),
+            dma((6,)),
             dma((S,)),
             regular,
             pltpu.SemaphoreType.REGULAR((max(1, C - 2),)),
-            dma((2, units)),
+            dma((units + S,)),
             dma((units,)),
             dma((units,)),
-            dma((units,)),
-            dma((R // 2, block_units)),
-            dma((R,)),
-            dma((R,)),
-            dma((R,)),
-            dma((R,)),
-            dma((C,)),
-            dma((C,)),
-            dma((R,)),
-            dma(()),
-            dma((g1,)),
-            dma((g1,)),
-            dma((R,)),
-            dma((R,)),
-            dma((D,)),
-            dma((D,)),
+            dma((R // 2 * block_units,)),
+            dma((max(1, R // 2 - 1), block_units)),
             dma((2,)),
             dma((2,)),
-            dma((C, feature_tiles)),
-            dma((2, feature_tiles)),
-        ] + [dma((g1,))] * 4,
+            dma(()),
+            dma(()),
+            dma(()),
+            dma(()),
+            dma((R // 2,)),
+            dma(()),
+            dma(()),
+            dma(()),
+            dma(()),
+            dma(()),
+            dma(()),
+            dma(()),
+            dma((2,)),
+            dma((2,)),
+            dma((C,)),
+            dma((2,)),
+        ] + [dma(())] * 4,
         compiler_params=pltpu.CompilerParams(
             collective_id=0, has_side_effects=True, vmem_limit_bytes=VMEM_LIMIT
         ),
@@ -837,6 +862,14 @@
         tokens.reshape(S, sub, features), frozen_weight, input_adapter_factor,
         output_adapter_factor, magnitude.reshape(1, cols), cotangent, sequence_lengths,
     )
+    results = [pltpu.with_memory_space_constraint(x, pltpu.VMEM) for x in results]
+    projected, grad_mag, factor_grad, grad_b = pl.pallas_call(
+        hand_over_kernel,
+        out_shape=tuple(jax.ShapeDtypeStruct(x.shape, x.dtype) for x in results),
+        in_specs=[vmem] * len(results),
+        out_specs=(hbm,) * len(results),
+        scratch_shapes=[dma((len(results),))],
+    )(*results)
     return projected, grad_mag.reshape(cols), factor_grad, grad_b
 
 

time: 93.4 us -> 89.4 us (0.957)
  local copies, waits for them, and re-layouts: 2.88 us -> 0 us
  Pallas kernels: 89.7 us -> 88.6 us
    unnamed x4 -> x0, local copies, waits for them, and re-layouts: 2.88 us -> none
    pallas_call x1, Pallas kernels: 89.7 us -> 87.5 us  [per_device(): pl.pallas_call(functools.partial(adapter_kernel, D, C, R, S, L), out_shap...]
    pallas_call x0 -> x1, Pallas kernels: none -> 1.09 us  [per_device(): pl.pallas_call(hand_over_kernel, out_shape=tuple((jax.ShapeDtypeStruct(x....]
where the time goes in v2:
time: 89.4 us; the launch traced here: 89.3 us
  Pallas kernels  88.6 us (99%)
    pallas_call x1, Pallas kernels, per_device(): pl.pallas_call(functools.partial(adapter_kernel, D, C, R, S, L), out_shap...  87.5 us

profile of v2, /device:TPU:0, one launch (start us, length us, event | category | flops | bytes accessed | tf_op | source)
XLA Modules:
  0.0 89.3 jit_solution(7373427878748425960)
XLA Ops:
  0.6 87.5 %shard_map.102 = (bf16[256,2048]{1,0:T(8,128)(2,1)S(1)}, f32[1,2048]{1,0:T(1,128)S(1)}, f32[16,2048]{1,0:T(8,128)S(1)}, f32[16,2048]{1,0:T(8,128)S(1)}) custom-call(bf16[4,64,2048]{2,1,0:T(8,128)(2,1)} %bitcast.3, bf16[2048,2048]{1,0:T(8,128)(2,1)} %w_hbm.1, bf16[16,2048]{1,0:T(8,128)(2,1)} %a_hbm.1, bf16[16,2048]{1,0:T(8,128)(2,1)} %b_hbm.1, ...), custom_call_target="tpu_custom_call" | custom-call | tf_op jit(solution)/shard_map/pallas_call | solution.py:779
  88.2 1.1 %shard_map.103 = (bf16[256,2048]{1,0:T(8,128)(2,1)}, f32[1,2048]{1,0:T(1,128)}, f32[16,2048]{1,0:T(8,128)}, f32[16,2048]{1,0:T(8,128)}) custom-call(bf16[256,2048]{1,0:T(8,128)(2,1)S(1)} %get-tuple-element.12.refs_0_, f32[1,2048]{1,0:T(1,128)S(1)} %get-tuple-element.13.refs_1_, f32[16,2048]{1,0:T(8,128)S(1)} %get-tuple-element.14.refs_2_, ...), custom_call_target="tpu_custom_call" | custom-call | tf_op jit(solution)/shard_map/pallas_call | solution.py:866

commit v3 on v2

--- a/solution.py
+++ b/solution.py
@@ -12,6 +12,8 @@
 MESH = pl.DeviceIdType.MESH
 LANES = 128
 FEATURE_TILE = 512
+TURN = 256
+PIECES = 4
 VMEM_LIMIT = 56 * 1024 * 1024
 
 
@@ -29,10 +31,10 @@
     D, C, R, S, L,
     tok, w_hbm, a_hbm, b_hbm, magnitude_hbm, cot_hbm, lengths_hbm,
     projected, grad_mag, factor_grad, grad_b,
-    lengths, wx, gath, sb, pin, xin, pb, st_in, st_pair, a_ref, b_ref, magnitude, apad, bpad, acc, own_sum, pg, cot, late_cot,
+    lengths, wx, wt, gath, sb, pin, xin, pb, st_in, st_pair, a_ref, b_ref, magnitude, apad, bpad, acc, own_sum, pg, cot, late_cot,
     row_weight, late_weight, down_in, down_all, merged_factor, col_norm, col_scale, coefficient_scale,
     scale_in, back_in, back_rows, bsum, bsum_all, box1, fsum, fsum_in, message, line_in, line_out, end_out, end_in,
-    load_sem, tok_sem, plane_sem, line_sem, gsend, grecv, ssend, precv, xrecv, stsend, strecv,
+    load_sem, tok_sem, plane_sem, line_sem, gsend, grecv, qsend, qrecv, ssend, precv, xrecv, stsend, strecv,
     dn_send, dn_recv, dz_send, dz_recv, late_send, late_recv, sc_send, sc_recv, bk_send, bk_recv,
     fs_send, fs_recv, ln_send, ln_recv, end_send, end_recv, r1a, r1b, r1c, r1d,
 ):
@@ -121,19 +123,33 @@
 
     def hop(u, direction):
         target = z - 1 if direction == 0 else z + 1
-        slot = u if direction == 0 else jnp.where(u // S == z, units + u % S, u)
-        return remote(gath.at[u], gath.at[u], gsend.at[slot], grecv.at[u], {"col": target})
+        return remote(gath.at[u], gath.at[u], gsend.at[direction], grecv.at[u], {"col": target})
+
+    ends = (z == 0) | (z == C - 1)
+    piece = features // PIECES
+
+    def hop_piece(u, j):
+        view = gath.at[u, :, pl.ds(j * piece, piece)]
+        origin = jnp.where(u // S == 0, 0, 1)
+        target = jnp.clip(jnp.where(u // S == 0, z + 1, z - 1), 0, C - 1)
+        return remote(view, view, qsend.at[origin], qrecv.at[origin, j], {"col": target})
 
     for s in range(S):
         load_tok(s).wait()
-
-        @pl.when(z > 0)
+        whole = jnp.logical_not(ends) if s == S - 1 else True
+
+        @pl.when((z > 0) & whole)
         def _():
             hop(z * S + s, 0).start()
 
-        @pl.when(z < C - 1)
+        @pl.when((z < C - 1) & whole)
         def _():
             hop(z * S + s, 1).start()
+
+    @pl.when(ends)
+    def _():
+        for j in range(PIECES):
+            hop_piece(z * S + S - 1, j).start()
 
     for i in range(1, D):
         signal(plane_sem, {"dp": (d + i) % D})
@@ -240,7 +256,9 @@
         for i in range(1, R):
             down = down + down_in[i]
         down_all[z] = down.astype(bf16)
-        loop(C, lambda i: spread_copy(i, z).start())
+        @pl.when(r == z * S // block_units)
+        def _():
+            loop(C, lambda i: spread_copy(i, z).start())
 
     near = jnp.minimum(z, C - 1 - z)
 
@@ -261,11 +279,11 @@
 
     def pair_copy(u):
         slot = u // block_units // 2 * block_units + u % block_units
-        return remote(sb.at[u], pin.at[u], ssend.at[u], precv.at[slot], {"row": p * 2 + (1 - q)})
+        return remote(sb.at[u], pin.at[u], ssend.at[0], precv.at[slot], {"row": p * 2 + (1 - q)})
 
     def far_copy(u, owner_pair):
         return remote(
-            sb.at[u], xin.at[p, u % block_units], ssend.at[u],
+            sb.at[u], xin.at[p, u % block_units], ssend.at[1],
             xrecv.at[(p - owner_pair + pairs) % pairs - 1, u % block_units],
             {"row": owner_pair * 2 + q},
         )
@@ -373,7 +391,15 @@
             back_copy(i, r).start()
 
     def middle():
-        settle(down_all.at[pl.ds(0, C - 1)], dz_recv, {"row": partner}).wait_recv()
+        @pl.when(z // chunks != r)
+        def _():
+            settle(down_all.at[pl.ds(0, chunks)], dz_recv, {"row": partner}).wait_recv()
+
+        if chunks > 1:
+            @pl.when(z // chunks == r)
+            def _():
+                settle(down_all.at[pl.ds(0, chunks - 1)], dz_recv, {"row": partner}).wait_recv()
+
         for start, width in tiles:
             span = pl.ds(start, width)
             total = jnp.zeros((rank_rows, width), f32)
@@ -423,7 +449,9 @@
         u = c * S + s
         owner = u // block_units
 
-        @pl.when(k >= S)
+        split = (k >= S) & (s == S - 1) & ((c == 0) | (c == C - 1))
+
+        @pl.when((k >= S) & jnp.logical_not(split))
         def _():
             hop(u, 0).wait_recv()
 
@@ -436,9 +464,27 @@
                 hop(u, 0).start()
 
         slot = k % 2
-        for start, width in tiles:
-            span = pl.ds(start, width)
-            pb[slot, :, span] = jnp.dot(gath[u], wx[:, span], preferred_element_type=f32)
+
+        @pl.when(jnp.logical_not(split))
+        def _():
+            for start, width in tiles:
+                span = pl.ds(start, width)
+                pb[slot, :, span] = jnp.dot(gath[u], wx[:, span], preferred_element_type=f32)
+
+        @pl.when(split)
+        def _():
+            for j in range(PIECES):
+                hop_piece(u, j).wait_recv()
+
+                @pl.when(((c == 0) & (z < C - 1)) | ((c != 0) & (z > 0)))
+                def _():
+                    hop_piece(u, j).start()
+
+                part = pl.ds(j * piece, piece)
+                for start, width in tiles:
+                    span = pl.ds(start, width)
+                    product = jnp.dot(gath[u, :, part], wx[part, span], preferred_element_type=f32)
+                    pb[slot, :, span] = product if j == 0 else pb[slot, :, span] + product
 
         @pl.when(k >= units - L)
         def _():
@@ -499,7 +545,7 @@
             for i in range(1, pairs):
                 other = (p + i) % pairs
                 remote(
-                    sb.at[v], xin.at[other, v], ssend.at[v], xrecv.at[i - 1, v], {"row": other * 2 + q}
+                    sb.at[v], xin.at[other, v], ssend.at[1], xrecv.at[i - 1, v], {"row": other * 2 + q}
                 ).wait_recv()
             rows = pl.ds(pl.multiple_of(v * sub, sub), sub)
             weight = row_weight[rows, 0:1]
@@ -533,6 +579,15 @@
         def _():
             pair_stats()
 
+        turned = k - (units - 1 - features // TURN)
+
+        @pl.when(ends & (turned >= 0) & (turned < features // TURN))
+        def _():
+            per_tile = FEATURE_TILE // TURN
+            rows = pl.ds(pl.multiple_of(turned * TURN, TURN), TURN)
+            lanes = pl.ds(pl.multiple_of(turned % per_tile * TURN, TURN), TURN)
+            wt[turned // per_tile, :, lanes] = wx[rows, :].T
+
         if C > 2:
             @pl.when(k == 2)
             def _():
@@ -593,7 +648,6 @@
         group_copy(i, d).start()
     combine(units - 1)
 
-    ends = (z == 0) | (z == C - 1)
     side = jnp.where(z == 0, 0, 1)
 
     def end_copy(i, t):
@@ -619,29 +673,35 @@
     coefficient = scale_grad * coefficient_scale[...]
     scaled = (b_ref[...].astype(f32) * coefficient).astype(bf16)
     cross = contract_product(scaled, b_ref[...], 1, 1)
-    for t, (start, width) in enumerate(feature_tiles):
+    if D > 1:
+        settle(fsum_in.at[pl.ds(0, D - 1)], fs_recv, {"row": partner}).wait_recv()
+
+    def term(t, product):
+        start, width = feature_tiles[t]
         span = pl.ds(start, width)
-        total = contract_product(scaled, wx[span, :], 1, 1) + jnp.dot(
+        total = product + jnp.dot(
             cross, a_ref[:, span].astype(f32),
             precision=highest_precision, preferred_element_type=f32,
         )
         total = total + fsum[:, span]
-        if t == 0 and D > 1:
-            settle(fsum_in.at[pl.ds(0, D - 1)], fs_recv, {"row": partner}).wait_recv()
         for i in range(1, D):
             total = total + fsum_in[(d - i + D) % D, :, span].astype(f32)
         message[:, span] = total
-
-        @pl.when(ends)
-        def _():
-            end_out[t] = message[:, span].astype(bf16)
-            for i in range(C - 1, 1, -1):
-                end_copy(i, t).start()
+        return total
 
     @pl.when(ends)
     def _():
         for t in range(len(feature_tiles)):
-            end_copy(1, t).start()
+            end_out[t] = term(t, jnp.dot(scaled, wt[t], preferred_element_type=f32)).astype(bf16)
+            end_copy(C - 1, t).start()
+        for i in range(C - 2, 0, -1):
+            for t in range(len(feature_tiles)):
+                end_copy(i, t).start()
+
+    @pl.when(jnp.logical_not(ends))
+    def _():
+        for t, (start, width) in enumerate(feature_tiles):
+            term(t, contract_product(scaled, wx[pl.ds(start, width), :], 1, 1))
 
     if C > 2:
         @pl.when((z > 0) & (z < C - 1))
@@ -672,7 +732,11 @@
     settle(scale_in.at[pl.ds(0, g1 - 1)], sc_send, device1(1)).wait_send()
     settle(back_in.at[pl.ds(0, R - 1)], bk_send, {"row": partner}).wait_send()
     settle(down_in.at[pl.ds(0, R - 1)], dn_send, {"row": partner}).wait_send()
-    settle(down_all.at[pl.ds(0, C - 1)], dz_send, {"row": partner}).wait_send()
+
+    @pl.when(r == z * S // block_units)
+    def _():
+        settle(down_all.at[pl.ds(0, C - 1)], dz_send, {"row": partner}).wait_send()
+
     if D > 1:
         settle(fsum_in.at[pl.ds(0, D - 1)], fs_send, {"row": partner}).wait_send()
 
@@ -689,25 +753,18 @@
     def _():
         late_near().wait_send()
 
-    def drain(u, carry):
-        c = u // S
-        owner = u // block_units
-
-        @pl.when((owner % 2 != q) | (owner // 2 != p))
-        def _():
-            pair_copy(u).wait_send()
-
-        @pl.when((c <= z) & (z < C - 1))
-        def _():
-            hop(u, 1).wait_send()
-
-        @pl.when((c >= z) & (z > 0))
-        def _():
-            hop(u, 0).wait_send()
-
-        return carry
-
-    lax.fori_loop(0, units, drain, 0)
+    settle(sb.at[pl.ds(0, units // 2)], ssend.at[0], {"row": partner}).wait_send()
+    if pairs > 1:
+        settle(sb.at[pl.ds(0, block_units * (pairs - 1))], ssend.at[1], {"row": partner}).wait_send()
+    for i in range(C):
+        @pl.when(z == i)
+        def _():
+            if i > 0:
+                settle(gath.at[pl.ds(0, (C - i) * S - 1)], gsend.at[0], {"row": partner}).wait_send()
+                settle(gath.at[0], qsend.at[1], {"row": partner}).wait_send()
+            if i < C - 1:
+                settle(gath.at[pl.ds(0, (i + 1) * S - 1)], gsend.at[1], {"row": partner}).wait_send()
+                settle(gath.at[0], qsend.at[0], {"row": partner}).wait_send()
 
     if C > 2:
         @pl.when(z == 0)
@@ -789,6 +846,7 @@
         scratch_shapes=[
             pltpu.SMEM(sequence_lengths.shape, jnp.int32),
             pltpu.VMEM((features, cols), bf16),
+            pltpu.VMEM((feature_tiles, cols, features // feature_tiles), bf16),
             pltpu.VMEM((units, sub, features), bf16),
             pltpu.VMEM((units, sub, cols), bf16),
             pltpu.VMEM((units, sub, cols), bf16),
@@ -831,9 +889,11 @@
             dma((S,)),
             regular,
             pltpu.SemaphoreType.REGULAR((max(1, C - 2),)),
-            dma((units + S,)),
+            dma((2,)),
             dma((units,)),
-            dma((units,)),
+            dma((2,)),
+            dma((2, PIECES)),
+            dma((2,)),
             dma((R // 2 * block_units,)),
             dma((max(1, R // 2 - 1), block_units)),
             dma((2,)),

time: 89.4 us -> 87.2 us (0.975)
  Pallas kernels: 88.6 us -> 86.4 us
    pallas_call x1, Pallas kernels: 87.5 us -> 85.3 us  [per_device(): pl.pallas_call(functools.partial(adapter_kernel, D, C, R, S, L), out_shap...]
where the time goes in v3:
time: 87.2 us; the launch traced here: 87 us
  Pallas kernels  86.4 us (99%)
    pallas_call x1, Pallas kernels, per_device(): pl.pallas_call(functools.partial(adapter_kernel, D, C, R, S, L), out_shap...  85.3 us

profile of v3, /device:TPU:0, one launch (start us, length us, event | category | flops | bytes accessed | tf_op | source)
XLA Modules:
  0.0 87.0 jit_solution(8397133665912842644)
XLA Ops:
  0.6 85.3 %shard_map.102 = (bf16[256,2048]{1,0:T(8,128)(2,1)S(1)}, f32[1,2048]{1,0:T(1,128)S(1)}, f32[16,2048]{1,0:T(8,128)S(1)}, f32[16,2048]{1,0:T(8,128)S(1)}) custom-call(bf16[4,64,2048]{2,1,0:T(8,128)(2,1)} %bitcast.3, bf16[2048,2048]{1,0:T(8,128)(2,1)} %w_hbm.1, bf16[16,2048]{1,0:T(8,128)(2,1)} %a_hbm.1, bf16[16,2048]{1,0:T(8,128)(2,1)} %b_hbm.1, ...), custom_call_target="tpu_custom_call" | custom-call | tf_op jit(solution)/shard_map/pallas_call | solution.py:836
  85.9 1.1 %shard_map.103 = (bf16[256,2048]{1,0:T(8,128)(2,1)}, f32[1,2048]{1,0:T(1,128)}, f32[16,2048]{1,0:T(8,128)}, f32[16,2048]{1,0:T(8,128)}) custom-call(bf16[256,2048]{1,0:T(8,128)(2,1)S(1)} %get-tuple-element.12.refs_0_, f32[1,2048]{1,0:T(1,128)S(1)} %get-tuple-element.13.refs_1_, f32[16,2048]{1,0:T(8,128)S(1)} %get-tuple-element.14.refs_2_, ...), custom_call_target="tpu_custom_call" | custom-call | tf_op jit(solution)/shard_map/pallas_call | solution.py:926

commit v4 on v3

--- a/solution.py
+++ b/solution.py
@@ -13,7 +13,7 @@
 LANES = 128
 FEATURE_TILE = 512
 TURN = 256
-PIECES = 4
+PIECES = 8
 VMEM_LIMIT = 56 * 1024 * 1024
 
 
@@ -33,10 +33,10 @@
     projected, grad_mag, factor_grad, grad_b,
     lengths, wx, wt, gath, sb, pin, xin, pb, st_in, st_pair, a_ref, b_ref, magnitude, apad, bpad, acc, own_sum, pg, cot, late_cot,
     row_weight, late_weight, down_in, down_all, merged_factor, col_norm, col_scale, coefficient_scale,
-    scale_in, back_in, back_rows, bsum, bsum_all, box1, fsum, fsum_in, message, line_in, line_out, end_out, end_in,
+    scale_in, back_in, back_rows, back_far, bsum, bsum_all, box1, fsum, fsum_in, message, line_in, line_out, end_out, end_in, cross_out, cross_in,
     load_sem, tok_sem, plane_sem, line_sem, gsend, grecv, qsend, qrecv, ssend, precv, xrecv, stsend, strecv,
     dn_send, dn_recv, dz_send, dz_recv, late_send, late_recv, sc_send, sc_recv, bk_send, bk_recv,
-    fs_send, fs_recv, ln_send, ln_recv, end_send, end_recv, r1a, r1b, r1c, r1d,
+    fs_send, fs_recv, ln_send, ln_recv, end_send, end_recv, bf_send, bf_recv, cx_send, cx_recv, r1a, r1b, r1c, r1d,
 ):
     z = lax.axis_index("col")
     r = lax.axis_index("row")
@@ -299,6 +299,11 @@
 
     def back_copy(i, piece):
         return remote(back_in.at[piece], back_in.at[piece], bk_send, bk_recv, {"row": (r + i) % R})
+
+    def far_back_copy():
+        unit = far_chunk * S + S - 1
+        rows = pl.ds(pl.multiple_of(unit % block_units * sub, sub), sub)
+        return remote(back_rows.at[unit // block_units, rows, :], back_far, bf_send, bf_recv, {"col": C - 1 - z})
 
     def scale_copy(i, piece):
         return remote(scale_in.at[piece], scale_in.at[piece], sc_send, sc_recv, device1(i))
@@ -531,7 +536,9 @@
         u = unit_of(k)
         block = u // block_units
         rows = pl.ds(pl.multiple_of((u % block_units) * sub, sub), sub)
-        back = back_rows[block, rows, :]
+        add_term(u, back_rows[block, rows, :])
+
+    def add_term(u, back):
         for start, width in feature_tiles:
             span = pl.ds(start, width)
             fsum[:, span] += contract_product(back, gath[u, :, span], 0, 0)[0:rank_rows]
@@ -568,7 +575,16 @@
 
         lax.fori_loop(first, last, turn, 0)
 
+    def group_copy(i, piece):
+        return remote(fsum_in.at[piece], fsum_in.at[piece], fs_send, fs_recv, {"dp": (d + i) % D})
+
+    def share_term():
+        fsum_in[d] = fsum[...].astype(bf16)
+        for i in range(1, D):
+            group_copy(i, d).start()
+
     fsum[...] = jnp.zeros_like(fsum)
+    cross_out[...] = jnp.zeros_like(cross_out)
 
     def step(k, carry):
         @pl.when(k > 0)
@@ -619,12 +635,25 @@
             for j in range(R):
                 back_rows[j] = contract_product(back_in[j], one, 0, 0).astype(bf16)
 
+            @pl.when(ends)
+            def _():
+                far_back_copy().start()
+
         @pl.when(k >= catch_up)
         def _():
             done = rate * (k - catch_up)
             each(jnp.minimum(done, k - 1), jnp.minimum(done + rate, k), factor_term)
             each(jnp.minimum(done, k - 2), jnp.minimum(done + rate, k - 1), finish)
 
+        @pl.when((k == units - 2) & ends)
+        def _():
+            far_back_copy().wait_recv()
+            add_term(z * S + S - 1, back_far[...])
+
+        @pl.when((k == units - 1) & ends)
+        def _():
+            share_term()
+
         @pl.when(k == catch_up + 1)
         def _():
             pass_late()
@@ -638,14 +667,11 @@
 
     lax.fori_loop(0, units, step, 0)
 
-    factor_term(units - 1)
-
-    def group_copy(i, piece):
-        return remote(fsum_in.at[piece], fsum_in.at[piece], fs_send, fs_recv, {"dp": (d + i) % D})
-
-    fsum_in[d] = fsum[...].astype(bf16)
-    for i in range(1, D):
-        group_copy(i, d).start()
+    @pl.when(jnp.logical_not(ends))
+    def _():
+        factor_term(units - 1)
+        share_term()
+
     combine(units - 1)
 
     side = jnp.where(z == 0, 0, 1)
@@ -672,28 +698,39 @@
         scale_grad = scale_grad + scale_in[j]
     coefficient = scale_grad * coefficient_scale[...]
     scaled = (b_ref[...].astype(f32) * coefficient).astype(bf16)
-    cross = contract_product(scaled, b_ref[...], 1, 1)
     if D > 1:
         settle(fsum_in.at[pl.ds(0, D - 1)], fs_recv, {"row": partner}).wait_recv()
 
     def term(t, product):
         start, width = feature_tiles[t]
         span = pl.ds(start, width)
-        total = product + jnp.dot(
-            cross, a_ref[:, span].astype(f32),
-            precision=highest_precision, preferred_element_type=f32,
-        )
-        total = total + fsum[:, span]
+        total = product + fsum[:, span]
         for i in range(1, D):
             total = total + fsum_in[(d - i + D) % D, :, span].astype(f32)
         message[:, span] = total
         return total
 
+    def add_cross(cross):
+        for start, width in feature_tiles:
+            span = pl.ds(start, width)
+            message[:, span] += jnp.dot(
+                cross, a_ref[:, span].astype(f32),
+                precision=highest_precision, preferred_element_type=f32,
+            )
+
+    def cross_copy(i):
+        target = jnp.where(z == 0, i, C - 1 - i)
+        return remote(cross_out, cross_in.at[side], cx_send, cx_recv.at[side], {"col": target})
+
     @pl.when(ends)
     def _():
         for t in range(len(feature_tiles)):
             end_out[t] = term(t, jnp.dot(scaled, wt[t], preferred_element_type=f32)).astype(bf16)
             end_copy(C - 1, t).start()
+            if t == 0:
+                cross_out[:, 0:rank_rows] = contract_product(scaled, b_ref[...], 1, 1)
+                for i in range(C - 1, 0, -1):
+                    cross_copy(i).start()
         for i in range(C - 2, 0, -1):
             for t in range(len(feature_tiles)):
                 end_copy(i, t).start()
@@ -702,26 +739,38 @@
     def _():
         for t, (start, width) in enumerate(feature_tiles):
             term(t, contract_product(scaled, wx[pl.ds(start, width), :], 1, 1))
+        add_cross(contract_product(scaled, b_ref[...], 1, 1))
+
+    def drain_stream(direction):
+        for i in range(C):
+            count = (C - i) * S - 1 if direction == 0 else (i + 1) * S - 1
+            if 0 <= i + 2 * direction - 1 < C:
+                @pl.when(z == i)
+                def _():
+                    settle(gath.at[pl.ds(0, count)], gsend.at[direction], {"row": partner}).wait_send()
+                    settle(gath.at[0], qsend.at[1 - direction], {"row": partner}).wait_send()
 
     if C > 2:
         @pl.when((z > 0) & (z < C - 1))
         def _():
             own = message[...]
+            more = ((z < C - 2), (z > 1))
             for direction in (0, 1):
-                more = (z < C - 2) if direction == 0 else (z > 1)
-
-                @pl.when(more)
+                @pl.when(jnp.logical_not(more[direction]))
+                def _():
+                    line_out[direction] = own.astype(bf16)
+                    drain_stream(direction)
+                    line_copy(direction).start()
+
+            for direction in (0, 1):
+                @pl.when(more[direction])
                 def _():
                     line_copy(direction).wait_recv()
                     incoming = line_in[direction].astype(f32)
                     line_out[direction] = (own + incoming).astype(bf16)
                     message[...] += incoming
-
-                @pl.when(jnp.logical_not(more))
-                def _():
-                    line_out[direction] = own.astype(bf16)
-
-                line_copy(direction).start()
+                    drain_stream(direction)
+                    line_copy(direction).start()
 
     each(units - 2, units, finish)
     grad_mag[...] = scale_grad / col_norm[...]
@@ -756,15 +805,12 @@
     settle(sb.at[pl.ds(0, units // 2)], ssend.at[0], {"row": partner}).wait_send()
     if pairs > 1:
         settle(sb.at[pl.ds(0, block_units * (pairs - 1))], ssend.at[1], {"row": partner}).wait_send()
-    for i in range(C):
-        @pl.when(z == i)
-        def _():
-            if i > 0:
-                settle(gath.at[pl.ds(0, (C - i) * S - 1)], gsend.at[0], {"row": partner}).wait_send()
-                settle(gath.at[0], qsend.at[1], {"row": partner}).wait_send()
-            if i < C - 1:
-                settle(gath.at[pl.ds(0, (i + 1) * S - 1)], gsend.at[1], {"row": partner}).wait_send()
-                settle(gath.at[0], qsend.at[0], {"row": partner}).wait_send()
+
+    @pl.when(ends)
+    def _():
+        drain_stream(0)
+        drain_stream(1)
+
 
     if C > 2:
         @pl.when(z == 0)
@@ -777,6 +823,16 @@
             line_copy(1).wait_recv()
             message[...] += line_in[1].astype(f32)
 
+    for j in (0, 1):
+        @pl.when(z != j * (C - 1))
+        def _():
+            remote(cross_out, cross_in.at[j], cx_send, cx_recv.at[j], {"row": partner}).wait_recv()
+            add_cross(cross_in[j, :, 0:rank_rows])
+
+    @pl.when(ends)
+    def _():
+        add_cross(cross_out[:, 0:rank_rows])
+
     @pl.when(z > 0)
     def _():
         end_arrived(0)
@@ -789,6 +845,8 @@
 
     @pl.when(ends)
     def _():
+        far_back_copy().wait_send()
+        settle(cross_in.at[pl.ds(0, C - 1)], cx_send, {"row": partner}).wait_send()
         for i in range(C - 1, 0, -1):
             settle(end_out, end_send.at[i], {"row": partner}).wait_send()
 
@@ -875,6 +933,7 @@
             pltpu.VMEM((g1, 1, cols), f32),
             pltpu.VMEM((R, rank_rows, block_rows), bf16),
             pltpu.VMEM((R, block_rows, LANES), bf16),
+            pltpu.VMEM((sub, LANES), bf16),
             pltpu.VMEM((rank_rows, cols), f32),
             pltpu.VMEM((rank_rows, cols), f32),
             pltpu.VMEM((g1, rank_rows, max(LANES, cols // g1)), f32),
@@ -885,6 +944,8 @@
             pltpu.VMEM((2, rank_rows, features), bf16),
             pltpu.VMEM((feature_tiles, rank_rows, features // feature_tiles), bf16),
             pltpu.VMEM((2, feature_tiles, rank_rows, features // feature_tiles), bf16),
+            pltpu.VMEM((rank_rows, LANES), f32),
+            pltpu.VMEM((max(2, C - 1), rank_rows, LANES), f32),
             dma((6,)),
             dma((S,)),
             regular,
@@ -913,6 +974,10 @@
             dma((2,)),
             dma((2,)),
             dma((C,)),
+            dma((2,)),
+            dma(()),
+            dma(()),
+            dma(()),
             dma((2,)),
         ] + [dma(())] * 4,
         compiler_params=pltpu.CompilerParams(

time: 87.2 us -> 87 us (level)
  no operation moved by 1% of the time
where the time goes in v4:
time: 87 us; the launch traced here: 86.8 us
  Pallas kernels  86.2 us (99%)
    pallas_call x1, Pallas kernels, per_device(): pl.pallas_call(functools.partial(adapter_kernel, D, C, R, S, L), out_shap...  85.1 us

profile of v4, /device:TPU:0, one launch (start us, length us, event | category | flops | bytes accessed | tf_op | source)
XLA Modules:
  0.0 86.8 jit_solution(8454734841087961093)
XLA Ops:
  0.6 85.1 %shard_map.102 = (bf16[256,2048]{1,0:T(8,128)(2,1)S(1)}, f32[1,2048]{1,0:T(1,128)S(1)}, f32[16,2048]{1,0:T(8,128)S(1)}, f32[16,2048]{1,0:T(8,128)S(1)}) custom-call(bf16[4,64,2048]{2,1,0:T(8,128)(2,1)} %bitcast.3, bf16[2048,2048]{1,0:T(8,128)(2,1)} %w_hbm.1, bf16[16,2048]{1,0:T(8,128)(2,1)} %a_hbm.1, bf16[16,2048]{1,0:T(8,128)(2,1)} %b_hbm.1, ...), custom_call_target="tpu_custom_call" | custom-call | tf_op jit(solution)/shard_map/pallas_call | solution.py:894
  85.7 1.1 %shard_map.103 = (bf16[256,2048]{1,0:T(8,128)(2,1)}, f32[1,2048]{1,0:T(1,128)}, f32[16,2048]{1,0:T(8,128)}, f32[16,2048]{1,0:T(8,128)}) custom-call(bf16[256,2048]{1,0:T(8,128)(2,1)S(1)} %get-tuple-element.12.refs_0_, f32[1,2048]{1,0:T(1,128)S(1)} %get-tuple-element.13.refs_1_, f32[16,2048]{1,0:T(8,128)S(1)} %get-tuple-element.14.refs_2_, ...), custom_call_target="tpu_custom_call" | custom-call | tf_op jit(solution)/shard_map/pallas_call | solution.py:991

commit v5 on v4

--- a/solution.py
+++ b/solution.py
@@ -635,7 +635,7 @@
             for j in range(R):
                 back_rows[j] = contract_product(back_in[j], one, 0, 0).astype(bf16)
 
-            @pl.when(ends)
+            @pl.when(z == C - 1)
             def _():
                 far_back_copy().start()
 
@@ -645,12 +645,12 @@
             each(jnp.minimum(done, k - 1), jnp.minimum(done + rate, k), factor_term)
             each(jnp.minimum(done, k - 2), jnp.minimum(done + rate, k - 1), finish)
 
-        @pl.when((k == units - 2) & ends)
+        @pl.when((k == units - 2) & (z == 0))
         def _():
             far_back_copy().wait_recv()
             add_term(z * S + S - 1, back_far[...])
 
-        @pl.when((k == units - 1) & ends)
+        @pl.when((k == units - 1) & (z == C - 1))
         def _():
             share_term()
 
@@ -667,7 +667,7 @@
 
     lax.fori_loop(0, units, step, 0)
 
-    @pl.when(jnp.logical_not(ends))
+    @pl.when(z != C - 1)
     def _():
         factor_term(units - 1)
         share_term()
@@ -845,7 +845,10 @@
 
     @pl.when(ends)
     def _():
-        far_back_copy().wait_send()
+        @pl.when(z == C - 1)
+        def _():
+            far_back_copy().wait_send()
+
         settle(cross_in.at[pl.ds(0, C - 1)], cx_send, {"row": partner}).wait_send()
         for i in range(C - 1, 0, -1):
             settle(end_out, end_send.at[i], {"row": partner}).wait_send()

time: 87 us -> 86.7 us (level)
  no operation moved by 1% of the time
where the time goes in v5:
time: 86.7 us; the launch traced here: 86.5 us
  Pallas kernels  85.9 us (99%)
    pallas_call x1, Pallas kernels, per_device(): pl.pallas_call(functools.partial(adapter_kernel, D, C, R, S, L), out_shap...  84.8 us

profile of v5, /device:TPU:0, one launch (start us, length us, event | category | flops | bytes accessed | tf_op | source)
XLA Modules:
  0.0 86.5 jit_solution(7146412077802143596)
XLA Ops:
  0.6 84.8 %shard_map.102 = (bf16[256,2048]{1,0:T(8,128)(2,1)S(1)}, f32[1,2048]{1,0:T(1,128)S(1)}, f32[16,2048]{1,0:T(8,128)S(1)}, f32[16,2048]{1,0:T(8,128)S(1)}) custom-call(bf16[4,64,2048]{2,1,0:T(8,128)(2,1)} %bitcast.3, bf16[2048,2048]{1,0:T(8,128)(2,1)} %w_hbm.1, bf16[16,2048]{1,0:T(8,128)(2,1)} %a_hbm.1, bf16[16,2048]{1,0:T(8,128)(2,1)} %b_hbm.1, ...), custom_call_target="tpu_custom_call" | custom-call | tf_op jit(solution)/shard_map/pallas_call | solution.py:897
  85.5 1.1 %shard_map.103 = (bf16[256,2048]{1,0:T(8,128)(2,1)}, f32[1,2048]{1,0:T(1,128)}, f32[16,2048]{1,0:T(8,128)}, f32[16,2048]{1,0:T(8,128)}) custom-call(bf16[256,2048]{1,0:T(8,128)(2,1)S(1)} %get-tuple-element.12.refs_0_, f32[1,2048]{1,0:T(1,128)S(1)} %get-tuple-element.13.refs_1_, f32[16,2048]{1,0:T(8,128)S(1)} %get-tuple-element.14.refs_2_, ...), custom_call_target="tpu_custom_call" | custom-call | tf_op jit(solution)/shard_map/pallas_call | solution.py:994
